TPU v7x, 32 devices: a whole 2x2x4 slice. The times are simulated.
32 devices in a mesh: fsdp: 4 (over y, core), tp: 4 (over z), rollout: 2 (over x).
Axes of the slice: x: 2, y: 2, z: 4, core: 2. Of those that a mesh axis runs over, the one named last changes fastest.
Arguments:
- weights: bfloat16 [2, 4096, 14336], P('rollout', 'fsdp', 'tp'), may hold values from -6 to 6
- gradient: bfloat16 [2, 4096, 14336], P('rollout', 'fsdp', 'tp'), may hold values from -6 to 6
- momentum: float32 [2, 4096, 14336], P('rollout', 'fsdp', 'tp'), may hold values from -90 to 90
- basis: float32 [2, 14336, 512], P('rollout', 'tp'), may hold values from -6 to 6
Outputs:
- weights_next: bfloat16 [2, 4096, 14336], P('rollout', 'fsdp', 'tp')
- momentum_next: float32 [2, 4096, 14336], P('rollout', 'fsdp', 'tp')
- basis_next: float32 [2, 14336, 512], P('rollout', 'tp')
- rollout_weights: bfloat16 [2, 4096, 14336], P(None, 'fsdp', 'tp')
All inputs are finite; a program needn't handle non-finite values.
Results may differ from a plain program's by a relative error of at most 0.013.
Values may be sent and summed in bfloat16 or wider, within the bound.
A program may use at most 192 MiB of HBM per device.

v0:
```python
import functools

import jax
import jax.numpy as jnp
from jax import lax
from jax.experimental import pallas as pl
from jax.experimental.pallas import tpu as pltpu
from jax.sharding import PartitionSpec as P


HIGH = lax.Precision.HIGHEST
BLOCK = 128


def dot_t(a, b):
    return lax.dot_general(
        a, b, (((1,), (1,)), ((), ())), precision=HIGH, preferred_element_type=jnp.float32
    )


def factor_kernel(g_ref, x_ref, a_ref, w_ref, s_ref, v_ref):
    n = g_ref.shape[0]
    nb = BLOCK
    a_ref[...] = g_ref[...]
    w_ref[...] = jnp.where(
        lax.broadcasted_iota(jnp.int32, (n, n), 0) == lax.broadcasted_iota(jnp.int32, (n, n), 1),
        1.0,
        0.0,
    ).astype(jnp.float32)
    lane = lax.broadcasted_iota(jnp.int32, (nb, nb), 1)
    sub = lax.broadcasted_iota(jnp.int32, (nb, nb), 0)
    lane_row = lax.broadcasted_iota(jnp.int32, (1, nb), 1)
    sub_col = lax.broadcasted_iota(jnp.int32, (nb, 1), 0)

    def step(k, carry):
        s = s_ref[...]
        v = v_ref[...]
        row = s_ref[pl.ds(k, 1), :]
        vrow = v_ref[pl.ds(k, 1), :]
        p = jnp.sum(jnp.where(lane_row == k, row, 0.0), axis=1, keepdims=True)
        col = jnp.sum(jnp.where(lane == k, s, 0.0), axis=1, keepdims=True)
        col = jnp.where(sub_col > k, col, 0.0)
        rp = 1.0 / p
        r = lax.rsqrt(p)
        r = r * (1.5 - 0.5 * p * r * r)
        s_ref[...] = s - col * (row * rp)
        v_ref[...] = v - col * (vrow * rp)
        v_ref[pl.ds(k, 1), :] = vrow * r
        return carry

    for lo in range(0, n, nb):
        hi = lo + nb
        s_ref[...] = a_ref[lo:hi, lo:hi]
        v_ref[...] = jnp.where(lane == sub, 1.0, 0.0).astype(jnp.float32)
        lax.fori_loop(0, nb, step, 0)
        inv = v_ref[...]
        x = jnp.dot(inv, w_ref[lo:hi, :hi], precision=HIGH, preferred_element_type=jnp.float32)
        x_ref[lo:hi, :hi] = x
        if hi < n:
            x_ref[lo:hi, hi:] = jnp.zeros((nb, n - hi), jnp.float32)
            panel = dot_t(a_ref[hi:, lo:hi], inv)
            a_ref[hi:, hi:] = a_ref[hi:, hi:] - dot_t(panel, panel)
            w_ref[hi:, :hi] = w_ref[hi:, :hi] - jnp.dot(
                panel, x, precision=HIGH, preferred_element_type=jnp.float32
            )


def inverse_factor(gram):
    n = gram.shape[0]
    return pl.pallas_call(
        factor_kernel,
        out_shape=jax.ShapeDtypeStruct((n, n), jnp.float32),
        in_specs=[pl.BlockSpec(memory_space=pltpu.VMEM)],
        out_specs=pl.BlockSpec(memory_space=pltpu.VMEM),
        scratch_shapes=[
            pltpu.VMEM((n, n), jnp.float32),
            pltpu.VMEM((n, n), jnp.float32),
            pltpu.VMEM((BLOCK, BLOCK), jnp.float32),
            pltpu.VMEM((BLOCK, BLOCK), jnp.float32),
        ],
        compiler_params=pltpu.CompilerParams(vmem_limit_bytes=16 << 20),
        cost_estimate=pl.CostEstimate(flops=2_000_000_000, bytes_accessed=8 * n * n, transcendentals=0),
        name="factor",
    )(gram)


def updated(w_ref, ortho_ref, right_ref, inv_ref):
    base = (right_ref[...].astype(jnp.float32) * inv_ref[...]).astype(jnp.bfloat16)
    update = lax.dot_general(
        ortho_ref[...], base, (((1,), (1,)), ((), ())), preferred_element_type=jnp.float32
    )
    return (w_ref[0].astype(jnp.float32) - 0.3 * update).astype(jnp.bfloat16)


def own_kernel(who_ref, w_ref, ortho_ref, right_ref, inv_ref, new_ref, both_ref):
    value = updated(w_ref, ortho_ref, right_ref, inv_ref)
    new_ref[0] = value
    both_ref[0] = value


def other_kernel(who_ref, w_ref, ortho_ref, right_ref, inv_ref, both_in, both_ref):
    both_ref[0] = updated(w_ref, ortho_ref, right_ref, inv_ref)


def pick(n, sizes):
    for s in sizes:
        if n % s == 0:
            return s
    return n


def apply_update(who, w, ortho, right, inv, both=None):
    _, rows, cols = w.shape
    rank = ortho.shape[1]
    tr = pick(rows, (512, 256, 128))
    tc = pick(cols, (896, 512, 256, 128))
    w_spec = pl.BlockSpec((1, tr, tc), lambda j, i, who: (0, i, j))
    both_spec = pl.BlockSpec((1, tr, tc), lambda j, i, who: (who[0], i, j))
    in_specs = [
        w_spec,
        pl.BlockSpec((tr, rank), lambda j, i, who: (i, 0)),
        pl.BlockSpec((tc, rank), lambda j, i, who: (j, 0)),
        pl.BlockSpec((1, rank), lambda j, i, who: (0, 0)),
    ]
    both_shape = jax.ShapeDtypeStruct((2, rows, cols), jnp.bfloat16)
    args = [who, w, ortho, right, inv]
    if both is None:
        kernel = own_kernel
        out_shape = (jax.ShapeDtypeStruct((1, rows, cols), jnp.bfloat16), both_shape)
        out_specs = (w_spec, both_spec)
        aliases = {}
    else:
        kernel = other_kernel
        in_specs.append(pl.BlockSpec(memory_space=pl.ANY))
        args.append(both)
        out_shape = both_shape
        out_specs = both_spec
        aliases = {5: 0}
    return pl.pallas_call(
        kernel,
        out_shape=out_shape,
        grid_spec=pltpu.PrefetchScalarGridSpec(
            num_scalar_prefetch=1,
            grid=(cols // tc, rows // tr),
            in_specs=in_specs,
            out_specs=out_specs,
        ),
        input_output_aliases=aliases,
        compiler_params=pltpu.CompilerParams(vmem_limit_bytes=32 << 20),
        cost_estimate=pl.CostEstimate(
            flops=2 * rows * cols * rank, bytes_accessed=6 * rows * cols, transcendentals=0
        ),
        name="apply_own" if both is None else "apply_other",
    )(*args)


def body(weights, gradient, momentum, basis):
    swap = functools.partial(lax.ppermute, axis_name="rollout", perm=[(0, 1), (1, 0)])
    me = lax.axis_index("rollout")
    cols = weights.shape[2] * lax.axis_size("tp")
    weights_other = swap(weights)
    blend = momentum[0] + gradient[0].astype(jnp.float32)
    share = lax.psum_scatter(
        jnp.dot(blend, basis[0], precision=lax.Precision.HIGH, preferred_element_type=jnp.float32),
        "tp",
        scatter_dimension=0,
        tiled=True,
    )
    gram = lax.psum(
        jnp.dot(share.T, share, precision=HIGH, preferred_element_type=jnp.float32), ("fsdp", "tp")
    )
    share, gram = lax.optimization_barrier((share, gram))
    left = lax.all_gather(share, "tp", axis=0, tiled=True)
    inverse = inverse_factor(gram)
    ortho = dot_t(left, inverse).astype(jnp.bfloat16)
    ortho_other = swap(ortho)
    partial_right = lax.dot_general(
        blend.astype(jnp.bfloat16),
        ortho,
        (((0,), (0,)), ((), ())),
        preferred_element_type=jnp.float32,
    )
    right = lax.psum(partial_right.astype(jnp.bfloat16), "fsdp")
    right_other = swap(right)
    wide = right.astype(jnp.float32)
    squares = lax.psum(jnp.sum(wide * wide, axis=0, keepdims=True), "tp")
    inv = lax.rsqrt(squares / cols + 1e-06)
    inv_other = swap(inv)
    weight_new, both = apply_update(me.reshape(1), weights, ortho, right, inv)
    moment_new = blend - 0.05 * lax.dot_general(
        ortho, right, (((1,), (1,)), ((), ())), preferred_element_type=jnp.float32
    )
    basis_new = wide * inv
    both = apply_update((1 - me).reshape(1), weights_other, ortho_other, right_other, inv_other, both)
    return (weight_new, moment_new[None], basis_new[None], both)


def solution(mesh):
    return jax.shard_map(
        body,
        mesh=mesh,
        in_specs=(
            P("rollout", "fsdp", "tp"),
            P("rollout", "fsdp", "tp"),
            P("rollout", "fsdp", "tp"),
            P("rollout", "tp", None),
        ),
        out_specs=(
            P("rollout", "fsdp", "tp"),
            P("rollout", "fsdp", "tp"),
            P("rollout", "tp", None),
            P(None, "fsdp", "tp"),
        ),
        check_vma=False,
    )
```

profile of v0, /device:TPU:0, one launch (start us, length us, event | category | flops | bytes accessed | tf_op | source)
XLA Modules:
  0.0 448.7 jit_solution(299463312511611119)
XLA Ops:
  7.2 0.0 reduce-scatter.2.cloned.1.call-start
  7.2 18.4 %fusion = f32[1024,512]{1,0:T(8,128)} fusion(f32[1,3584,512]{2,1,0:T(8,128)} %param.7, f32[1,1024,3584]{2,1,0:T(8,128)} %param.6, bf16[1,1024,3584]{2,1,0:T(8,128)(2,1)} %param.5), kind=kOutput, calls=%fused_computation.2 | convolution fusion | flops 11281629184 | bytes 31457280 | tf_op jit(solution)/shard_map/dot_general | solution.py:164
  25.6 0.0 reduce-scatter.2.cloned.1.call-update
  25.6 0.0 all-reduce.3.cloned.1.call-start
  25.7 46.5 %reduce-scatter.2.cloned.1.call-done = f32[256,512]{1,0:T(8,128)} async-done(((f32[1024,512]{1,0:T(8,128)}), f32[256,512]{1,0:T(8,128)}) %reduce-scatter.2.cloned.1.call-update) | async-done | bytes 524304 | tf_op jit(solution)/shard_map/reduce_scatter | solution.py:163
  72.2 3.2 fusion.8
  75.4 0.0 all-reduce.3.cloned.1.call-update
  75.4 0.0 all-gather.2.cloned.1.call-start
  75.4 93.8 %all-reduce.3.cloned.1.call-done.g_ref = f32[512,512]{1,0:T(8,128)} async-done(((f32[512,512]{1,0:T(8,128)}), f32[512,512]{1,0:T(8,128)}) %all-reduce.3.cloned.1.call-update) | async-done | bytes 1048592 | tf_op jit(solution)/shard_map/psum | solution.py:169
  169.2 0.0 all-gather.2.cloned.1.call-update
  169.2 0.2 all-reduce.5.cloned.1.call-start
  169.4 1.5 collective-permute-start
  171.0 1.2 copy-done.2
  172.2 55.6 %factor.1 = f32[512,512]{1,0:T(8,128)S(1)} custom-call(f32[512,512]{1,0:T(8,128)S(1)} %copy-done.2), custom_call_target="tpu_custom_call" | custom-call | flops 2000000000 | bytes 2097152 | tf_op jit(solution)/shard_map/factor/pallas_call | solution.py:70
  227.8 0.0 all-gather.2.cloned.1.call-done
  227.8 5.1 %convolution_convert_fusion.ortho_ref = bf16[1024,512]{1,0:T(8,128)(2,1)S(1)} fusion(f32[1024,512]{1,0:T(8,128)} %all-gather.2.cloned.1.call-done, f32[512,512]{1,0:T(8,128)S(1)} %factor.1), kind=kOutput, calls=%fused_computation.13 | convolution fusion | flops 3221749760 | bytes 4194304 | tf_op jit(solution)/shard_map/dot_general | solution.py:16
  232.9 14.5 %fusion.7 = bf16[3584,512]{1,0:T(8,128)(2,1)} fusion(bf16[1024,512]{1,0:T(8,128)(2,1)S(1)} %convolution_convert_fusion.ortho_ref, f32[1,1024,3584]{2,1,0:T(8,128)} %param.6, bf16[1,1024,3584]{2,1,0:T(8,128)(2,1)} %param.5), kind=kOutput, calls=%fused_computation.12 | convolution fusion | flops 3770941440 | bytes 26738688 | tf_op jit(solution)/shard_map/dot_general | solution.py:177
  247.3 0.0 all-reduce.5.cloned.1.call-update
  247.4 0.6 collective-permute-start.1
  248.0 74.7 %all-reduce.5.cloned.1.call-done.right_ref = bf16[3584,512]{1,0:T(8,128)(2,1)} async-done(((bf16[3584,512]{1,0:T(8,128)(2,1)}), bf16[3584,512]{1,0:T(8,128)(2,1)}) %all-reduce.5.cloned.1.call-update) | async-done | bytes 3670032 | tf_op jit(solution)/shard_map/psum | solution.py:183
  322.6 1.5 collective-permute-start.2
  324.1 2.9 fusion.3
  327.0 11.9 %psum.23 = f32[1,512]{1,0:T(1,128)S(1)} all-reduce(f32[1,512]{1,0:T(1,128)S(1)} %bitcast.29), channel_id=1, replica_groups=mesh['fsdp'=4,'tp'=4,'rollout'=2] {'tp'}, use_global_device_ids=true, to_apply=%region_4.0 | all-reduce | flops 512 | bytes 4096 | tf_op jit(solution)/shard_map/psum | solution.py:186
  338.9 0.6 collective-permute-start.3
  339.6 15.7 %fusion.2 = f32[1,1024,3584]{2,1,0:T(8,128)} fusion(bf16[1024,512]{1,0:T(8,128)(2,1)S(1)} %convolution_convert_fusion.ortho_ref, bf16[3584,512]{1,0:T(8,128)(2,1)} %all-reduce.5.cloned.1.call-done.right_ref, f32[1,1024,3584]{2,1,0:T(8,128)} %param.6, bf16[1,1024,3584]{2,1,0:T(8,128)(2,1)} %param.5), kind=kOutput, calls=%fused_computation.4 | convolution fusion | flops 3772776448 | bytes 41418752 | tf_op jit(solution)/shard_map/dot_general | solution.py:190
  355.3 4.1 fusion.4
  359.4 3.1 copy-done.1
  362.5 9.2 %apply_own.1 = (bf16[1,1024,3584]{2,1,0:T(8,128)(2,1)}, bf16[2,1024,3584]{2,1,0:T(8,128)(2,1)}) custom-call(s32[1]{0:T(128)} %bitcast.who_ref, bf16[1,1024,3584]{2,1,0:T(8,128)(2,1)S(1)} %copy-done.1, bf16[1024,512]{1,0:T(8,128)(2,1)S(1)} %convolution_convert_fusion.ortho_ref, bf16[3584,512]{1,0:T(8,128)(2,1)S(1)} %copy-done, f32[1,512]{1,0:T(1,128)S(1)} %add_rsqrt_fusion.inv_ref), custom_call_target="tpu_custom_call" | custom-call | flops 3758096384 | bytes 22020096 | tf_op jit(solution)/shard_map/apply_own/pallas_call | solution.py:139
  371.6 0.0 collective-permute-done.w_ref
  371.6 58.3 %collective-permute-done.3.inv_ref = f32[1,512]{1,0:T(1,128)S(1)} collective-permute-done((f32[1,512]{1,0:T(1,128)S(1)}, f32[1,512]{1,0:T(1,128)S(1)}, u32[]{:S(2)}, u32[]{:S(2)}) %collective-permute-start.3) | collective-permute-done | bytes 2080 | tf_op jit(solution)/shard_map/ppermute | solution.py:188
  429.9 0.0 collective-permute-done.2.right_ref
  429.9 12.3 %apply_other.1 = bf16[2,1024,3584]{2,1,0:T(8,128)(2,1)} custom-call(s32[1]{0:T(128)} %bitcast.7.who_ref, bf16[1,1024,3584]{2,1,0:T(8,128)(2,1)} %collective-permute-done.w_ref, bf16[1024,512]{1,0:T(8,128)(2,1)S(1)} %collective-permute-done.1.ortho_ref, bf16[3584,512]{1,0:T(8,128)(2,1)} %collective-permute-done.2.right_ref, ...), custom_call_target="tpu_custom_call", output_to_operand_aliasing={{}: (5, {})} | custom-call | flops 3758096384 | bytes 22020096 | tf_op jit(solution)/shard_map/apply_other/pallas_call | solution.py:139
  (6 shorter events, 0.0 us)
Async XLA Ops:
  7.2 65.0 %reduce-scatter.2.cloned.1.call-start = ((), (), s32[]{:S(2)}) async-start(), calls=%async_computation.1 | async-start | bytes 2621440 | tf_op jit(solution)/shard_map/reduce_scatter | solution.py:163
  25.6 143.6 %all-reduce.3.cloned.1.call-start = ((), (), s32[]{:S(2)}) async-start(), calls=%async_computation.2 | async-start | bytes 2097152 | tf_op jit(solution)/shard_map/psum | solution.py:169
  75.4 152.4 %all-gather.2.cloned.1.call-start = ((), (), s32[]{:S(2)}) async-start(), calls=%async_computation.3 | async-start | bytes 2621440 | tf_op jit(solution)/shard_map/all_gather | solution.py:173
  169.2 153.4 %all-reduce.5.cloned.1.call-start = ((), (), s32[]{:S(2)}) async-start(), calls=%async_computation.4 | async-start | bytes 7340032 | tf_op jit(solution)/shard_map/psum | solution.py:183
  169.4 202.2 %collective-permute-start = (bf16[1,1024,3584]{2,1,0:T(8,128)(2,1)}, bf16[1,1024,3584]{2,1,0:T(8,128)(2,1)}, u32[]{:S(2)}, u32[]{:S(2)}) collective-permute-start(bf16[1,1024,3584]{2,1,0:T(8,128)(2,1)} %w_ref.1), channel_id=1, source_target_pairs={{0,1},{1,0},{2,3},{3,2},{4,5},{5,4},{6,7},{7,6},{8,9},{9,8},{10,11... | collective-permute-start | bytes 22020104 | tf_op jit(solution)/shard_map/ppermute | solution.py:161
  171.0 1.2 copy-start.2
  247.4 124.3 %collective-permute-start.1 = (bf16[1024,512]{1,0:T(8,128)(2,1)S(1)}, bf16[1024,512]{1,0:T(8,128)(2,1)S(1)}, u32[]{:S(2)}, u32[]{:S(2)}) collective-permute-start(bf16[1024,512]{1,0:T(8,128)(2,1)S(1)} %convolution_convert_fusion.ortho_ref), channel_id=1, source_target_pairs={{0,1},{1,0},{2,3},{3,2},{4,5},{5,4},{6,7},{7,6},{8,9},{9,8},{10,11... | collective-permute-start | bytes 3145736 | tf_op jit(solution)/shard_map/ppermute | solution.py:176
  322.6 107.2 %collective-permute-start.2 = (bf16[3584,512]{1,0:T(8,128)(2,1)}, bf16[3584,512]{1,0:T(8,128)(2,1)}, u32[]{:S(2)}, u32[]{:S(2)}) collective-permute-start(bf16[3584,512]{1,0:T(8,128)(2,1)} %all-reduce.5.cloned.1.call-done.right_ref), channel_id=1, source_target_pairs={{0,1},{1,0},{2,3},{3,2},{4,5},{5,4},{6,7},{7,6},{8,9},{9,8},{10,11... | collective-permute-start | bytes 11010056 | tf_op jit(solution)/shard_map/ppermute | solution.py:184
  338.9 16.3 %copy-start = (bf16[3584,512]{1,0:T(8,128)(2,1)S(1)}, bf16[3584,512]{1,0:T(8,128)(2,1)}, u32[]{:S(2)}) copy-start(bf16[3584,512]{1,0:T(8,128)(2,1)} %all-reduce.5.cloned.1.call-done.right_ref) | copy-start | bytes 11010052
  338.9 90.9 %collective-permute-start.3 = (f32[1,512]{1,0:T(1,128)S(1)}, f32[1,512]{1,0:T(1,128)S(1)}, u32[]{:S(2)}, u32[]{:S(2)}) collective-permute-start(f32[1,512]{1,0:T(1,128)S(1)} %add_rsqrt_fusion.inv_ref), channel_id=1, source_target_pairs={{0,1},{1,0},{2,3},{3,2},{4,5},{5,4},{6,7},{7,6},{8,9},{9,8},{10,11... | collective-permute-start | bytes 6152 | tf_op jit(solution)/shard_map/ppermute | solution.py:188
  359.4 3.1 copy-start.1
Sparse Core Ops, SparseCore 0:
  25.8 46.3 reduce-scatter.1
  76.2 92.9 all-reduce.2
  170.8 44.8 all-gather.1
  247.5 75.1 all-reduce.4
where the time goes:
time: 449 us
  waiting for transfers between devices  273 us (61%)
  Pallas kernels  77 us (17%)
  matrix products  56.8 us (13%)
  between operations  13.8 us (3%)
  blocking collectives  11.9 us (3%)
  other arithmetic  7.02 us (2%)
  starting transfers between devices  4.57 us (1%)
    psum x1, waiting for transfers between devices, body(): lax.psum(jnp.dot(share.T, share, precision=HIGH, preferred_element_type=j...  93.8 us
    psum x1, waiting for transfers between devices, body(): right = lax.psum(partial_right.astype(jnp.bfloat16), 'fsdp')  74.7 us
    ppermute x1, waiting for transfers between devices, body(): inv_other = swap(inv)  58.3 us
    pallas_call x1, Pallas kernels, inverse_factor(): pl.pallas_call(factor_kernel, out_shape=jax.ShapeDtypeStruct((n, n), jnp....  55.6 us
    reduce_scatter x1, waiting for transfers between devices, body(): lax.psum_scatter(jnp.dot(blend, basis[0], precision=lax.Precision.HIGH, p...  46.5 us
    pallas_call x2, Pallas kernels, apply_update(): pl.pallas_call(kernel, out_shape=out_shape, grid_spec=pltpu.PrefetchScala...  21.5 us
    dot_general x1, matrix products, body(): jnp.dot(blend, basis[0], precision=lax.Precision.HIGH, preferred_element_...  18.4 us
    dot_general x1, matrix products, body(): lax.dot_general(ortho, right, (((1,), (1,)), ((), ())), preferred_element...  15.7 us
  transfers between devices with their start and end apart: 8, of which 4 were waited for; matrix products, arithmetic and copies ran while one was open for 9% of the time, Pallas kernels for 14%

commit v1 on v0

v1 whole, which is shorter than its diff:
```python
import functools

import jax
import jax.numpy as jnp
from jax import lax
from jax.experimental import pallas as pl
from jax.experimental.pallas import tpu as pltpu
from jax.sharding import PartitionSpec as P


HIGH = lax.Precision.HIGHEST
BLOCK = 128
STRIP = 32
MESH = pl.DeviceIdType.MESH


def dot_t(a, b):
    return lax.dot_general(
        a, b, (((1,), (1,)), ((), ())), precision=HIGH, preferred_element_type=jnp.float32
    )


def pick(n, sizes):
    for s in sizes:
        if n % s == 0:
            return s
    return n


def remote(src, dst, send, recv, **where):
    return pltpu.make_async_remote_copy(
        src_ref=src, dst_ref=dst, send_sem=send, recv_sem=recv, device_id=where, device_id_type=MESH
    )


def greet(nf, nt):
    f, t = lax.axis_index("fsdp"), lax.axis_index("tp")
    barrier = pltpu.get_barrier_semaphore()
    n = nf * nt
    me = f * nt + t

    def one(i, carry):
        q = lax.rem(me + 1 + i, n)
        pl.semaphore_signal(
            barrier, inc=1, device_id={"fsdp": q // nt, "tp": lax.rem(q, nt)}, device_id_type=MESH
        )
        return carry

    lax.fori_loop(0, n - 1, one, 0)
    pl.semaphore_wait(barrier, n - 1)


def factor_block(s_ref, v_ref):
    nb = BLOCK
    tile = STRIP
    lane = lax.broadcasted_iota(jnp.int32, (tile, nb), 1)
    sub = lax.broadcasted_iota(jnp.int32, (tile, nb), 0)

    def strip(j, carry):
        rows = pl.ds(pl.multiple_of(j * tile, tile), tile)
        s = s_ref[rows, :]
        v = v_ref[rows, :]
        turned = pltpu.roll(s, lax.rem(nb - j * tile, nb), 1)
        cols = [jnp.broadcast_to(turned[:, i : i + 1], (tile, nb)) for i in range(tile)]
        pivot = jnp.ones((tile, nb), jnp.float32)
        recip = jnp.ones((tile, nb), jnp.float32)
        for i in range(tile):
            p = jnp.broadcast_to(cols[i][i : i + 1, :], (tile, nb))
            rp = 1.0 / p
            pivot = jnp.where(sub == i, p, pivot)
            recip = jnp.where(sub == i, rp, recip)
            if i < tile - 1:
                by = jnp.where(sub > i, cols[i] * rp, 0.0)
                for m in range(i + 1, tile):
                    cols[m] = cols[m] - by * jnp.broadcast_to(cols[m][i : i + 1, :], (tile, nb))
                s = s - by * jnp.broadcast_to(s[i : i + 1, :], (tile, nb))
                v = v - by * jnp.broadcast_to(v[i : i + 1, :], (tile, nb))
        below = jnp.where(lane >= (j + 1) * tile, s * recip, 0.0)
        change = lax.dot_general(
            below,
            jnp.concatenate([s, v], axis=1),
            (((0,), (0,)), ((), ())),
            precision=HIGH,
            preferred_element_type=jnp.float32,
        )
        s_ref[...] = s_ref[...] - change[:, :nb]
        v_ref[...] = v_ref[...] - change[:, nb:]
        r = lax.rsqrt(pivot)
        r = r * (1.5 - 0.5 * pivot * r * r)
        v_ref[rows, :] = v * r
        return carry

    lax.fori_loop(0, nb // tile, strip, 0)


def factor(a_ref, x_ref, w_ref, s_ref, v_ref):
    n = a_ref.shape[0]
    nb = BLOCK
    w_ref[...] = jnp.where(
        lax.broadcasted_iota(jnp.int32, (n, n), 0) == lax.broadcasted_iota(jnp.int32, (n, n), 1),
        1.0,
        0.0,
    ).astype(jnp.float32)
    lane = lax.broadcasted_iota(jnp.int32, (nb, nb), 1)
    sub = lax.broadcasted_iota(jnp.int32, (nb, nb), 0)

    for lo in range(0, n, nb):
        hi = lo + nb
        s_ref[...] = a_ref[lo:hi, lo:hi]
        v_ref[...] = jnp.where(lane == sub, 1.0, 0.0).astype(jnp.float32)
        factor_block(s_ref, v_ref)
        inv = v_ref[...]
        x = jnp.dot(inv, w_ref[lo:hi, :hi], precision=HIGH, preferred_element_type=jnp.float32)
        x_ref[lo:hi, :hi] = x
        if hi < n:
            x_ref[lo:hi, hi:] = jnp.zeros((nb, n - hi), jnp.float32)
            panel = dot_t(a_ref[hi:, lo:hi], inv)
            a_ref[hi:, hi:] = a_ref[hi:, hi:] - dot_t(panel, panel)
            w_ref[hi:, :hi] = w_ref[hi:, :hi] - jnp.dot(
                panel, x, precision=HIGH, preferred_element_type=jnp.float32
            )


def mid_kernel(
    nf, nt, cuts, part_ref, ortho_ref,
    left, rbuf, lbuf, gpart, gmate, pieces, gram, inverse, work, s_ref, v_ref,
    rs_send, rs_recv, mate_send, mate_recv, p_send, p_recv, q_send, q_recv, ag_send, ag_recv,
):
    f, t = lax.axis_index("fsdp"), lax.axis_index("tp")
    core = lax.rem(f, 2)
    mate = f + 1 - 2 * core
    rows, rank = part_ref.shape
    share = rows // nt
    sub = share // cuts
    half = rank // 2
    group = (nf // 2) * nt
    owners = min(group, half // 8)
    piece = half // owners
    p = (f // 2) * nt + t

    greet(nf, nt)

    def chunk(d, c):
        return part_ref.at[pl.ds(pl.multiple_of(d * share + c * sub, sub), sub)]

    def moves(i):
        c = lax.rem(i, cuts)
        k = i // cuts
        return nt - 1 - k, k, c

    def to_right(src, d, c):
        return remote(src, rbuf.at[d, c], rs_send.at[0, d, c], rs_recv.at[0, d, c], tp=t + 1)

    def to_left(src, e, c):
        return remote(src, lbuf.at[e, c], rs_send.at[1, e, c], rs_recv.at[1, e, c], tp=t - 1)

    def scatter(i, carry):
        d, e, c = moves(i)

        @pl.when(jnp.logical_and(t < d, t == 0))
        def _():
            to_right(chunk(d, c), d, c).start()

        @pl.when(jnp.logical_and(t > e, t == nt - 1))
        def _():
            to_left(chunk(e, c), e, c).start()

        @pl.when(jnp.logical_and(t < d, t > 0))
        def _():
            to_right(rbuf.at[d, c], d, c).wait_recv()
            rbuf[d, c] = rbuf[d, c] + chunk(d, c)[...]
            to_right(rbuf.at[d, c], d, c).start()

        @pl.when(jnp.logical_and(t > e, t < nt - 1))
        def _():
            to_left(lbuf.at[e, c], e, c).wait_recv()
            lbuf[e, c] = lbuf[e, c] + chunk(e, c)[...]
            to_left(lbuf.at[e, c], e, c).start()

        return carry

    lax.fori_loop(0, (nt - 1) * cuts, scatter, 0)

    def mine(c, carry):
        here = pl.ds(pl.multiple_of(t * share + c * sub, sub), sub)
        left[here, :] = part_ref[here, :]

        @pl.when(t > 0)
        def _():
            to_right(rbuf.at[t, c], t, c).wait_recv()
            left[here, :] = left[here, :] + rbuf[t, c]

        @pl.when(t < nt - 1)
        def _():
            to_left(lbuf.at[t, c], t, c).wait_recv()
            left[here, :] = left[here, :] + lbuf[t, c]

        return carry

    lax.fori_loop(0, cuts, mine, 0)

    here = pl.ds(pl.multiple_of(t * share, share), share)
    own = left[here, :]
    gpart[...] = lax.dot_general(
        own, own, (((0,), (0,)), ((), ())), precision=HIGH, preferred_element_type=jnp.float32
    )
    keep = pl.ds(pl.multiple_of(core * half, half), half)
    give = pl.ds(pl.multiple_of((1 - core) * half, half), half)
    pair = remote(gpart.at[give], gmate, mate_send.at[0], mate_recv.at[0], fsdp=mate)
    pair.start()
    pair.wait_recv()
    gmate[...] = gmate[...] + gpart[keep, :]

    def at(q):
        return {"fsdp": 2 * (q // nt) + core, "tp": lax.rem(q, nt)}

    def part_of(q):
        return gmate.at[pl.ds(pl.multiple_of(q * piece, piece), piece)]

    def send_piece(i, carry):
        q = lax.rem(p + 1 + i, group)

        @pl.when(q < owners)
        def _():
            remote(part_of(q), pieces.at[p], p_send.at[q], p_recv.at[p], **at(q)).start()

        return carry

    lax.fori_loop(0, group - 1, send_piece, 0)

    def final_of(q):
        return gram.at[pl.ds(pl.multiple_of(core * half + q * piece, piece), piece)]

    @pl.when(p < owners)
    def _():
        pieces[p] = part_of(p)[...]

        def got(i, carry):
            q = lax.rem(p + 1 + i, group)
            remote(part_of(p), pieces.at[q], p_send.at[0], p_recv.at[q], **at(q)).wait_recv()
            return carry

        lax.fori_loop(0, group - 1, got, 0)
        final_of(p)[...] = lax.fori_loop(
            1, group, lambda q, acc: acc + pieces[q], pieces[0]
        )

        def spread(i, carry):
            q = lax.rem(p + 1 + i, group)
            remote(final_of(p), final_of(p), q_send.at[q], q_recv.at[p], **at(q)).start()
            return carry

        lax.fori_loop(0, group - 1, spread, 0)

    def got_final(q, carry):
        @pl.when(q != p)
        def _():
            remote(final_of(q), final_of(q), q_send.at[0], q_recv.at[q], **at(q)).wait_recv()

        return carry

    lax.fori_loop(0, owners, got_final, 0)
    other = remote(gram.at[keep], gram.at[keep], mate_send.at[1], mate_recv.at[1], fsdp=mate)
    other.start()

    def gather(i, carry):
        q = lax.rem(t + 1 + i, nt)
        remote(left.at[here], left.at[here], ag_send.at[q], ag_recv.at[t], tp=q).start()
        return carry

    lax.fori_loop(0, nt - 1, gather, 0)
    remote(gram.at[give], gram.at[give], mate_send.at[1], mate_recv.at[1], fsdp=mate).wait_recv()
    pair.wait_send()
    gpart[...] = gram[...]
    factor(gpart, inverse, work, s_ref, v_ref)

    def ortho_of(i, carry):
        q = lax.rem(t + i, nt)
        there = pl.ds(pl.multiple_of(q * share, share), share)

        @pl.when(i > 0)
        def _():
            remote(left.at[there], left.at[there], ag_send.at[0], ag_recv.at[q], tp=q).wait_recv()

        ortho_ref[there, :] = dot_t(left[there, :], inverse[...]).astype(jnp.bfloat16)
        return carry

    lax.fori_loop(0, nt, ortho_of, 0)

    def drain(i, carry):
        d, e, c = moves(i)

        @pl.when(t < d)
        def _():
            to_right(rbuf.at[d, c], d, c).wait_send()

        @pl.when(t > e)
        def _():
            to_left(lbuf.at[e, c], e, c).wait_send()

        return carry

    lax.fori_loop(0, (nt - 1) * cuts, drain, 0)
    other.wait_send()

    def drain_pieces(i, carry):
        q = lax.rem(p + 1 + i, group)

        @pl.when(q < owners)
        def _():
            remote(part_of(q), pieces.at[p], p_send.at[q], p_recv.at[p], **at(q)).wait_send()

        @pl.when(p < owners)
        def _():
            remote(final_of(p), final_of(p), q_send.at[q], q_recv.at[p], **at(q)).wait_send()

        return carry

    lax.fori_loop(0, group - 1, drain_pieces, 0)

    def drain_gather(i, carry):
        q = lax.rem(t + 1 + i, nt)
        remote(left.at[here], left.at[here], ag_send.at[q], ag_recv.at[t], tp=q).wait_send()
        return carry

    lax.fori_loop(0, nt - 1, drain_gather, 0)


def mid(part, nf, nt):
    rows, rank = part.shape
    share = rows // nt
    cuts = 2 if (share // 2) % 8 == 0 else 1
    sub = share // cuts
    half = rank // 2
    group = (nf // 2) * nt
    owners = min(group, half // 8)
    f32 = jnp.float32
    dma = pltpu.SemaphoreType.DMA
    return pl.pallas_call(
        functools.partial(mid_kernel, nf, nt, cuts),
        out_shape=jax.ShapeDtypeStruct((rows, rank), jnp.bfloat16),
        in_specs=[pl.BlockSpec(memory_space=pltpu.VMEM)],
        out_specs=pl.BlockSpec(memory_space=pltpu.VMEM),
        scratch_shapes=[
            pltpu.VMEM((rows, rank), f32),
            pltpu.VMEM((nt, cuts, sub, rank), f32),
            pltpu.VMEM((nt, cuts, sub, rank), f32),
            pltpu.VMEM((rank, rank), f32),
            pltpu.VMEM((half, rank), f32),
            pltpu.VMEM((group, half // owners, rank), f32),
            pltpu.VMEM((rank, rank), f32),
            pltpu.VMEM((rank, rank), f32),
            pltpu.VMEM((rank, rank), f32),
            pltpu.VMEM((BLOCK, BLOCK), f32),
            pltpu.VMEM((BLOCK, BLOCK), f32),
            dma((2, nt, cuts)), dma((2, nt, cuts)),
            dma((2,)), dma((2,)),
            dma((group,)), dma((group,)),
            dma((group,)), dma((group,)),
            dma((nt,)), dma((nt,)),
        ],
        compiler_params=pltpu.CompilerParams(
            vmem_limit_bytes=40 << 20, collective_id=0, has_side_effects=True
        ),
        cost_estimate=pl.CostEstimate(
            flops=30_000_000_000, bytes_accessed=8 * rank * rank, transcendentals=0
        ),
        name="mid",
    )(part)


def right_kernel(
    nf, nt, cuts, cols, part_ref, right_ref, inv_ref,
    mbuf, sbuf, ybuf, sqs,
    m_send, m_recv, y_send, y_recv, g_send, g_recv, w_send, w_recv, sq_send, sq_recv,
):
    f, t = lax.axis_index("fsdp"), lax.axis_index("tp")
    core = lax.rem(f, 2)
    y = f // 2
    ny = nf // 2
    mate = f + 1 - 2 * core
    half = part_ref.shape[0] // 2
    quarter = half // ny
    sub = quarter // cuts
    n = nf * nt
    me = f * nt + t
    f32, b16 = jnp.float32, jnp.bfloat16

    greet(nf, nt)

    def rows_of(h, q, c):
        return pl.ds(pl.multiple_of(h * half + q * quarter + c * sub, sub), sub)

    def order(i):
        return lax.rem(y + 1 + i // cuts, ny), lax.rem(i, cuts)

    def to_mate(q, c):
        return remote(
            part_ref.at[rows_of(1 - core, q, c)], mbuf.at[q, c], m_send.at[q, c], m_recv.at[q, c],
            fsdp=mate,
        )

    def start_mate(i, carry):
        q, c = order(i)
        to_mate(q, c).start()
        return carry

    lax.fori_loop(0, ny * cuts, start_mate, 0)

    def to_peer(q, c):
        return remote(
            sbuf.at[q, c], ybuf.at[y, c], y_send.at[q, c], y_recv.at[y, c], fsdp=2 * q + core
        )

    def pair_sum(i, carry):
        q, c = order(i)
        to_mate(q, c).wait_recv()
        sbuf[q, c] = (part_ref[rows_of(core, q, c), :].astype(f32) + mbuf[q, c].astype(f32)).astype(b16)
        to_peer(q, c).start()
        return carry

    lax.fori_loop(0, (ny - 1) * cuts, pair_sum, 0)

    def spread(q, c):
        rows = rows_of(core, y, c)
        return remote(
            right_ref.at[rows], right_ref.at[rows], g_send.at[q, c], g_recv.at[y, c], fsdp=2 * q + core
        )

    def to_other_core(q, c):
        rows = rows_of(core, q, c)
        return remote(
            right_ref.at[rows], right_ref.at[rows], w_send.at[q, c], w_recv.at[q, c], fsdp=mate
        )

    sqs[me] = jnp.zeros_like(sqs[me])

    def reduce(c, carry):
        to_mate(y, c).wait_recv()
        total = part_ref[rows_of(core, y, c), :].astype(f32) + mbuf[y, c].astype(f32)

        def add(i, acc):
            q = lax.rem(y + 1 + i, ny)
            remote(
                sbuf.at[y, c], ybuf.at[q, c], y_send.at[q, c], y_recv.at[q, c], fsdp=2 * q + core
            ).wait_recv()
            return acc + ybuf[q, c].astype(f32)

        total = lax.fori_loop(0, ny - 1, add, total)
        rows = rows_of(core, y, c)
        right_ref[rows, :] = total.astype(b16)
        sqs[me] = sqs[me] + jnp.sum((total * total).reshape(sub // 8, 8, total.shape[1]), axis=0)

        def send(i, carry):
            spread(lax.rem(y + 1 + i, ny), c).start()
            return carry

        lax.fori_loop(0, ny - 1, send, 0)
        to_other_core(y, c).start()
        return carry

    lax.fori_loop(0, cuts, reduce, 0)

    def to_all(q):
        return remote(
            sqs.at[me], sqs.at[me], sq_send.at[q], sq_recv.at[me], fsdp=q // nt, tp=lax.rem(q, nt)
        )

    def start_squares(i, carry):
        to_all(lax.rem(me + 1 + i, n)).start()
        return carry

    lax.fori_loop(0, n - 1, start_squares, 0)

    def forward(i, carry):
        q, c = order(i)
        rows = rows_of(core, q, c)
        remote(
            right_ref.at[rows], right_ref.at[rows], g_send.at[q, c], g_recv.at[q, c], fsdp=2 * q + core
        ).wait_recv()
        to_other_core(q, c).start()
        return carry

    lax.fori_loop(0, (ny - 1) * cuts, forward, 0)

    def got_square(i, carry):
        q = lax.rem(me + 1 + i, n)
        remote(
            sqs.at[q], sqs.at[q], sq_send.at[q], sq_recv.at[q], fsdp=q // nt, tp=lax.rem(q, nt)
        ).wait_recv()
        return carry

    lax.fori_loop(0, n - 1, got_square, 0)
    total = lax.fori_loop(1, n, lambda q, acc: acc + sqs[q], sqs[0])
    meansq = jnp.sum(total, axis=0, keepdims=True) / cols
    inv_ref[...] = lax.rsqrt(meansq + 1e-06)

    def finish(i, carry):
        q, c = order(i)
        rows = rows_of(1 - core, q, c)
        remote(
            right_ref.at[rows], right_ref.at[rows], w_send.at[q, c], w_recv.at[q, c], fsdp=mate
        ).wait_recv()
        to_mate(q, c).wait_send()
        to_other_core(q, c).wait_send()

        @pl.when(q != y)
        def _():
            to_peer(q, c).wait_send()
            spread(q, c).wait_send()

        return carry

    lax.fori_loop(0, ny * cuts, finish, 0)

    def drain_squares(i, carry):
        to_all(lax.rem(me + 1 + i, n)).wait_send()
        return carry

    lax.fori_loop(0, n - 1, drain_squares, 0)


def sub_blocks(quarter):
    for cuts in (4, 2):
        if quarter % (16 * cuts) == 0:
            return cuts
    return 1


def right_sum(part, nf, nt, cols):
    mine, rank = part.shape
    ny = nf // 2
    quarter = mine // nf
    cuts = sub_blocks(quarter)
    sub = quarter // cuts
    n = nf * nt
    b16 = jnp.bfloat16
    dma = pltpu.SemaphoreType.DMA
    return pl.pallas_call(
        functools.partial(right_kernel, nf, nt, cuts, cols),
        out_shape=(
            jax.ShapeDtypeStruct((mine, rank), b16),
            jax.ShapeDtypeStruct((1, rank), jnp.float32),
        ),
        in_specs=[pl.BlockSpec(memory_space=pltpu.VMEM)],
        out_specs=(pl.BlockSpec(memory_space=pltpu.VMEM), pl.BlockSpec(memory_space=pltpu.VMEM)),
        scratch_shapes=[
            pltpu.VMEM((ny, cuts, sub, rank), b16),
            pltpu.VMEM((ny, cuts, sub, rank), b16),
            pltpu.VMEM((ny, cuts, sub, rank), b16),
            pltpu.VMEM((n, 8, rank), jnp.float32),
            dma((ny, cuts)), dma((ny, cuts)),
            dma((ny, cuts)), dma((ny, cuts)),
            dma((ny, cuts)), dma((ny, cuts)),
            dma((ny, cuts)), dma((ny, cuts)),
            dma((n,)), dma((n,)),
        ],
        compiler_params=pltpu.CompilerParams(
            vmem_limit_bytes=40 << 20, collective_id=1, has_side_effects=True
        ),
        cost_estimate=pl.CostEstimate(
            flops=10_000_000_000, bytes_accessed=4 * mine * rank, transcendentals=0
        ),
        name="right_sum",
    )(part)


def spread_kernel(
    nf, nt, cuts, o_ref, r_ref, ortho_ref, right_ref,
    o_send, o_recv, g_send, g_recv, w_send, w_recv, here_sem,
):
    f, t = lax.axis_index("fsdp"), lax.axis_index("tp")
    core = lax.rem(f, 2)
    y = f // 2
    ny = nf // 2
    mate = f + 1 - 2 * core
    share = o_ref.shape[0]
    quarter = r_ref.shape[0]
    half = quarter * ny
    sub = quarter // cuts

    greet(nf, nt)

    def rows_of(h, q, c):
        return pl.ds(pl.multiple_of(h * half + q * quarter + c * sub, sub), sub)

    def mine(c):
        return r_ref.at[pl.ds(pl.multiple_of(c * sub, sub), sub)]

    def block(q):
        return pl.ds(pl.multiple_of(q * share, share), share)

    def order(i):
        return lax.rem(y + 1 + i // cuts, ny), lax.rem(i, cuts)

    def to_peer(q, c):
        return remote(
            mine(c), right_ref.at[rows_of(core, y, c)], g_send.at[q, c], g_recv.at[y, c],
            fsdp=2 * q + core,
        )

    def start_peer(i, carry):
        q, c = order(i)
        to_peer(q, c).start()
        return carry

    lax.fori_loop(0, (ny - 1) * cuts, start_peer, 0)

    def to_line(q):
        return remote(o_ref, ortho_ref.at[block(t)], o_send.at[q], o_recv.at[t], tp=q)

    def start_line(i, carry):
        to_line(lax.rem(t + 1 + i, nt)).start()
        return carry

    lax.fori_loop(0, nt - 1, start_line, 0)

    def own_to_mate(c):
        return remote(
            mine(c), right_ref.at[rows_of(core, y, c)], w_send.at[y, c], w_recv.at[y, c], fsdp=mate
        )

    def start_own(c, carry):
        own_to_mate(c).start()
        return carry

    lax.fori_loop(0, cuts, start_own, 0)
    first = pltpu.make_async_copy(o_ref, ortho_ref.at[block(t)], here_sem.at[0])
    second = pltpu.make_async_copy(
        r_ref, right_ref.at[pl.ds(pl.multiple_of(core * half + y * quarter, quarter), quarter)], here_sem.at[1]
    )
    first.start()
    second.start()

    def to_other_core(q, c):
        rows = rows_of(core, q, c)
        return remote(
            right_ref.at[rows], right_ref.at[rows], w_send.at[q, c], w_recv.at[q, c], fsdp=mate
        )

    def forward(i, carry):
        q, c = order(i)
        rows = rows_of(core, q, c)
        remote(mine(c), right_ref.at[rows], g_send.at[q, c], g_recv.at[q, c], fsdp=2 * q + core).wait_recv()
        to_other_core(q, c).start()
        return carry

    lax.fori_loop(0, (ny - 1) * cuts, forward, 0)

    def finish(i, carry):
        q, c = order(i)
        rows = rows_of(1 - core, q, c)
        remote(
            right_ref.at[rows], right_ref.at[rows], w_send.at[q, c], w_recv.at[q, c], fsdp=mate
        ).wait_recv()
        to_other_core(q, c).wait_send()

        @pl.when(q != y)
        def _():
            to_peer(q, c).wait_send()

        return carry

    lax.fori_loop(0, ny * cuts, finish, 0)

    def finish_line(i, carry):
        q = lax.rem(t + 1 + i, nt)
        remote(o_ref, ortho_ref.at[block(q)], o_send.at[q], o_recv.at[q], tp=q).wait_recv()
        to_line(q).wait_send()
        return carry

    lax.fori_loop(0, nt - 1, finish_line, 0)
    first.wait()
    second.wait()


def spread_other(ortho, right, nf, nt):
    share, rank = ortho.shape
    quarter = right.shape[0]
    ny = nf // 2
    cuts = sub_blocks(quarter)
    dma = pltpu.SemaphoreType.DMA
    vmem = pl.BlockSpec(memory_space=pltpu.VMEM)
    return pl.pallas_call(
        functools.partial(spread_kernel, nf, nt, cuts),
        out_shape=(
            jax.ShapeDtypeStruct((share * nt, rank), jnp.bfloat16),
            jax.ShapeDtypeStruct((quarter * nf, rank), jnp.bfloat16),
        ),
        in_specs=[vmem, vmem],
        out_specs=(vmem, vmem),
        scratch_shapes=[
            dma((nt,)), dma((nt,)),
            dma((ny, cuts)), dma((ny, cuts)),
            dma((ny, cuts)), dma((ny, cuts)),
            dma((2,)),
        ],
        compiler_params=pltpu.CompilerParams(
            vmem_limit_bytes=32 << 20, collective_id=2, has_side_effects=True
        ),
        cost_estimate=pl.CostEstimate(
            flops=5_000_000_000, bytes_accessed=4 * quarter * nf * rank, transcendentals=0
        ),
        name="spread_other",
    )(ortho, right)


def updated(w_ref, ortho_ref, right_ref, inv_ref):
    base = (right_ref[...].astype(jnp.float32) * inv_ref[...]).astype(jnp.bfloat16)
    update = lax.dot_general(
        ortho_ref[...], base, (((1,), (1,)), ((), ())), preferred_element_type=jnp.float32
    )
    return (w_ref[0].astype(jnp.float32) - 0.3 * update).astype(jnp.bfloat16)


def own_kernel(who_ref, w_ref, ortho_ref, right_ref, inv_ref, new_ref, both_ref):
    value = updated(w_ref, ortho_ref, right_ref, inv_ref)
    new_ref[0] = value
    both_ref[0] = value


def other_kernel(who_ref, w_ref, ortho_ref, right_ref, inv_ref, both_in, both_ref):
    both_ref[0] = updated(w_ref, ortho_ref, right_ref, inv_ref)


def apply_update(who, w, ortho, right, inv, both=None):
    _, rows, cols = w.shape
    rank = ortho.shape[1]
    tr = pick(rows, (512, 256, 128))
    tc = pick(cols, (896, 512, 256, 128))
    w_spec = pl.BlockSpec((1, tr, tc), lambda j, i, who: (0, i, j))
    both_spec = pl.BlockSpec((1, tr, tc), lambda j, i, who: (who[0], i, j))
    in_specs = [
        w_spec,
        pl.BlockSpec((tr, rank), lambda j, i, who: (i, 0)),
        pl.BlockSpec((tc, rank), lambda j, i, who: (j, 0)),
        pl.BlockSpec((1, rank), lambda j, i, who: (0, 0)),
    ]
    both_shape = jax.ShapeDtypeStruct((2, rows, cols), jnp.bfloat16)
    args = [who, w, ortho, right, inv]
    if both is None:
        kernel = own_kernel
        out_shape = (jax.ShapeDtypeStruct((1, rows, cols), jnp.bfloat16), both_shape)
        out_specs = (w_spec, both_spec)
        aliases = {}
    else:
        kernel = other_kernel
        in_specs.append(pl.BlockSpec(memory_space=pl.ANY))
        args.append(both)
        out_shape = both_shape
        out_specs = both_spec
        aliases = {5: 0}
    return pl.pallas_call(
        kernel,
        out_shape=out_shape,
        grid_spec=pltpu.PrefetchScalarGridSpec(
            num_scalar_prefetch=1,
            grid=(cols // tc, rows // tr),
            in_specs=in_specs,
            out_specs=out_specs,
        ),
        input_output_aliases=aliases,
        compiler_params=pltpu.CompilerParams(vmem_limit_bytes=32 << 20),
        cost_estimate=pl.CostEstimate(
            flops=2 * rows * cols * rank, bytes_accessed=6 * rows * cols, transcendentals=0
        ),
        name="apply_own" if both is None else "apply_other",
    )(*args)


def body(weights, gradient, momentum, basis):
    swap = functools.partial(lax.ppermute, axis_name="rollout", perm=[(0, 1), (1, 0)])
    me = lax.axis_index("rollout")
    f, t = lax.axis_index("fsdp"), lax.axis_index("tp")
    nf, nt = lax.axis_size("fsdp"), lax.axis_size("tp")
    cols = weights.shape[2] * nt
    weights_other = swap(weights)
    blend = momentum[0] + gradient[0].astype(jnp.float32)
    part = jnp.dot(blend, basis[0], precision=HIGH, preferred_element_type=jnp.float32)
    ortho = mid(part, nf, nt)
    rows = ortho.shape[0]
    partial_right = lax.dot_general(
        blend.astype(jnp.bfloat16),
        ortho,
        (((0,), (0,)), ((), ())),
        preferred_element_type=jnp.float32,
    ).astype(jnp.bfloat16)
    right, inv = right_sum(partial_right, nf, nt, cols)
    share = rows // nt
    quarter = right.shape[0] // nf
    ortho_piece = swap(lax.dynamic_slice_in_dim(ortho, t * share, share, 0))
    place = (f % 2) * (nf // 2) + f // 2
    right_piece = swap(lax.dynamic_slice_in_dim(right, place * quarter, quarter, 0))
    inv_other = swap(inv)
    weight_new, both = apply_update(me.reshape(1), weights, ortho, right, inv)
    moment_new = blend - 0.05 * lax.dot_general(
        ortho, right, (((1,), (1,)), ((), ())), preferred_element_type=jnp.float32
    )
    basis_new = right.astype(jnp.float32) * inv
    ortho_other, right_other = spread_other(ortho_piece, right_piece, nf, nt)
    both = apply_update((1 - me).reshape(1), weights_other, ortho_other, right_other, inv_other, both)
    return (weight_new, moment_new[None], basis_new[None], both)


def solution(mesh):
    return jax.shard_map(
        body,
        mesh=mesh,
        in_specs=(
            P("rollout", "fsdp", "tp"),
            P("rollout", "fsdp", "tp"),
            P("rollout", "fsdp", "tp"),
            P("rollout", "tp", None),
        ),
        out_specs=(
            P("rollout", "fsdp", "tp"),
            P("rollout", "fsdp", "tp"),
            P("rollout", "tp", None),
            P(None, "fsdp", "tp"),
        ),
        check_vma=False,
    )
```

time: 449 us -> 298 us (0.66)
  waiting for transfers between devices: 273 us -> 0.01 us
  Pallas kernels: 77 us -> 223 us
  between operations: 13.8 us -> 0.74 us
  blocking collectives: 11.9 us -> 0 us
    psum x2 -> x0, waiting for transfers between devices: 168 us -> none  [the longest x1 93.8 us: body(): lax.psum(jnp.dot(share.T, share, precision=HIGH, preferred_element_type=j...]
    pallas_call x1 -> x3, Pallas kernels: 55.6 us -> 203 us  [the longest x1 114 us: mid(): pl.pallas_call(functools.partial(mid_kernel, nf, nt, cuts), out_shape=jax...]
    ppermute x1, waiting for transfers between devices: 58.3 us -> 0.01 us  [body(): inv_other = swap(inv)]
    reduce_scatter x1 -> x0, waiting for transfers between devices: 46.5 us -> none  [body(): lax.psum_scatter(jnp.dot(blend, basis[0], precision=lax.Precision.HIGH, p...]
    psum x1 -> x0, blocking collectives: 11.9 us -> none  [body(): squares = lax.psum(jnp.sum(wide * wide, axis=0, keepdims=True), 'tp')]
    dot_general x3 -> x1, matrix products: 26.7 us -> 28.3 us  [body(): jnp.dot(blend, basis[0], precision=HIGH, preferred_element_type=jnp.float32)]
  transfers between devices with their start and end apart: 8 -> 4, of which waited for: 4 -> 0; matrix products, arithmetic and copies ran while one was open for 9% -> 21% of each run, Pallas kernels for 14% -> 71%
where the time goes in v1:
time: 298 us; the launch traced here: 297 us
  Pallas kernels  223 us (75%)
  matrix products  57.3 us (19%)
  local copies, waits for them, and re-layouts  7.03 us (2%)
  starting transfers between devices  5.73 us (2%)
  other arithmetic  4.1 us (1%)
    pallas_call x1, Pallas kernels, mid(): pl.pallas_call(functools.partial(mid_kernel, nf, nt, cuts), out_shape=jax...  114 us
    pallas_call x1, Pallas kernels, right_sum(): pl.pallas_call(functools.partial(right_kernel, nf, nt, cuts, cols), out_s...  63 us
    dot_general x1, matrix products, body(): jnp.dot(blend, basis[0], precision=HIGH, preferred_element_type=jnp.float32)  28.3 us
    pallas_call x1, Pallas kernels, spread_other(): pl.pallas_call(functools.partial(spread_kernel, nf, nt, cuts), out_shape=...  25.2 us
    pallas_call x2, Pallas kernels, apply_update(): pl.pallas_call(kernel, out_shape=out_shape, grid_spec=pltpu.PrefetchScala...  20 us
    dot_general x1, matrix products, body(): lax.dot_general(ortho, right, (((1,), (1,)), ((), ())), preferred_element...  15.8 us
    dot_general x1, matrix products, body(): lax.dot_general(blend.astype(jnp.bfloat16), ortho, (((0,), (0,)), ((), ()...  13.2 us
    unnamed x8, local copies, waits for them, and re-layouts  6.96 us
  transfers between devices with their start and end apart: 4, of which 0 were waited for; matrix products, arithmetic and copies ran while one was open for 21% of the time, Pallas kernels for 71%

profile of v1, /device:TPU:0, one launch (start us, length us, event | category | flops | bytes accessed | tf_op | source)
XLA Modules:
  0.0 297.5 jit_solution(173815991215355097)
XLA Ops:
  0.6 3.0 %collective-permute-start = (bf16[1,1024,3584]{2,1,0:T(8,128)(2,1)}, bf16[1,1024,3584]{2,1,0:T(8,128)(2,1)}, u32[]{:S(2)}, u32[]{:S(2)}) collective-permute-start(bf16[1,1024,3584]{2,1,0:T(8,128)(2,1)} %w_ref.1), channel_id=1, source_target_pairs={{0,1},{1,0},{2,3},{3,2},{4,5},{5,4},{6,7},{7,6},{8,9},{9,8},{10,11... | collective-permute-start | bytes 22020104 | tf_op jit(solution)/shard_map/ppermute | solution.py:777
  3.7 28.3 %fusion.part_ref = f32[1024,512]{1,0:T(8,128)S(1)} fusion(f32[1,3584,512]{2,1,0:T(8,128)} %param.7, f32[1,1024,3584]{2,1,0:T(8,128)} %param.6, bf16[1,1024,3584]{2,1,0:T(8,128)(2,1)} %param.5), kind=kOutput, calls=%fused_computation.2 | convolution fusion | flops 22555918336 | bytes 31457280 | tf_op jit(solution)/shard_map/dot_general | solution.py:779
  31.9 114.4 %mid.1.ortho_ref = bf16[1024,512]{1,0:T(8,128)(2,1)S(1)} custom-call(f32[1024,512]{1,0:T(8,128)S(1)} %fusion.part_ref), custom_call_target="tpu_custom_call" | custom-call | flops 30000001024 | bytes 2097152 | tf_op jit(solution)/shard_map/mid/pallas_call | solution.py:339
  146.3 13.2 %fusion.5.part_ref = bf16[3584,512]{1,0:T(8,128)(2,1)S(1)} fusion(bf16[1024,512]{1,0:T(8,128)(2,1)S(1)} %mid.1.ortho_ref, f32[1,1024,3584]{2,1,0:T(8,128)} %param.6, bf16[1,1024,3584]{2,1,0:T(8,128)(2,1)} %param.5), kind=kOutput, calls=%fused_computation.9 | convolution fusion | flops 3770941440 | bytes 26738688 | tf_op jit(solution)/shard_map/dot_general | solution.py:782
  159.6 63.0 %right_sum.1 = (bf16[3584,512]{1,0:T(8,128)(2,1)S(1)}, f32[1,512]{1,0:T(1,128)S(1)}) custom-call(bf16[3584,512]{1,0:T(8,128)(2,1)S(1)} %fusion.5.part_ref), custom_call_target="tpu_custom_call" | custom-call | flops 10000000000 | bytes 7340032 | tf_op jit(solution)/shard_map/right_sum/pallas_call | solution.py:539
  222.5 0.0 copy-start
  222.5 1.8 copy-done
  224.4 0.1 constant_dynamic-slice_fusion
  224.4 0.6 collective-permute-start.2
  225.1 1.6 collective-permute-start.1
  226.6 0.0 copy-start.1
  226.6 0.5 collective-permute-start.3
  227.2 15.8 %fusion.2 = f32[1,1024,3584]{2,1,0:T(8,128)} fusion(bf16[1024,512]{1,0:T(8,128)(2,1)S(1)} %mid.1.ortho_ref, bf16[3584,512]{1,0:T(8,128)(2,1)} %copy-done, f32[1,1024,3584]{2,1,0:T(8,128)} %param.6, bf16[1,1024,3584]{2,1,0:T(8,128)(2,1)} %param.5), kind=kOutput, calls=%fused_computation.4 | convolution fusion | flops 3772776448 | bytes 41418752 | tf_op jit(solution)/shard_map/dot_general | solution.py:796
  243.0 0.0 copy-done.1
  243.0 4.1 %multiply_bitcast_fusion = f32[1,3584,512]{2,1,0:T(8,128)} fusion(bf16[3584,512]{1,0:T(8,128)(2,1)S(1)} %copy-done.1, f32[512]{0:T(512)S(1)} %bitcast.23), kind=kLoop, calls=%fused_computation.8 | loop fusion | flops 3670016 | bytes 11012096 | tf_op jit(solution)/shard_map/broadcast_in_dim | solution.py:802
  247.1 0.0 copy-start.2
  247.1 2.0 copy-done.2
  249.1 0.0 copy-start.3
  249.1 3.1 %copy-done.3 = bf16[1,1024,3584]{2,1,0:T(8,128)(2,1)S(1)} copy-done((bf16[1,1024,3584]{2,1,0:T(8,128)(2,1)S(1)}, bf16[1,1024,3584]{2,1,0:T(8,128)(2,1)}, u32[]{:S(2)}) %copy-start.3) | copy-done | bytes 7340056
  252.2 9.2 %apply_own.1 = (bf16[1,1024,3584]{2,1,0:T(8,128)(2,1)}, bf16[2,1024,3584]{2,1,0:T(8,128)(2,1)}) custom-call(s32[1]{0:T(128)} %bitcast.who_ref, bf16[1,1024,3584]{2,1,0:T(8,128)(2,1)S(1)} %copy-done.3, bf16[1024,512]{1,0:T(8,128)(2,1)S(1)} %mid.1.ortho_ref, bf16[3584,512]{1,0:T(8,128)(2,1)S(1)} %copy-done.2, f32[1,512]{1,0:T(1,128)S(1)} %get-tuple-element.11.inv_ref), custom_call_target="tpu_custom_call" | custom-call | flops 3758096384 | bytes 22020096 | tf_op jit(solution)/shard_map/apply_own/pallas_call | solution.py:753
  261.4 0.0 collective-permute-done.1.o_ref
  261.4 0.0 collective-permute-done.2.r_ref
  261.4 25.2 %spread_other.1 = (bf16[1024,512]{1,0:T(8,128)(2,1)S(1)}, bf16[3584,512]{1,0:T(8,128)(2,1)S(1)}) custom-call(bf16[256,512]{1,0:T(8,128)(2,1)S(1)} %collective-permute-done.1.o_ref, bf16[896,512]{1,0:T(8,128)(2,1)S(1)} %collective-permute-done.2.r_ref), custom_call_target="tpu_custom_call" | custom-call | flops 5000000000 | bytes 7340032 | tf_op jit(solution)/shard_map/spread_other/pallas_call | solution.py:684
  286.6 0.0 collective-permute-done.3.inv_ref
  286.6 0.0 collective-permute-done.w_ref
  286.6 10.8 %apply_other.1 = bf16[2,1024,3584]{2,1,0:T(8,128)(2,1)} custom-call(s32[1]{0:T(128)} %bitcast.6.who_ref, bf16[1,1024,3584]{2,1,0:T(8,128)(2,1)} %collective-permute-done.w_ref, bf16[1024,512]{1,0:T(8,128)(2,1)S(1)} %get-tuple-element.13.ortho_ref, bf16[3584,512]{1,0:T(8,128)(2,1)S(1)} %get-tuple-element.14.right_ref, ...), custom_call_target="tpu_custom_call", output_to_operand_aliasing={{}: (5, {})} | custom-call | flops 3758096384 | bytes 22020096 | tf_op jit(solution)/shard_map/apply_other/pallas_call | solution.py:753
  (1 shorter events, 0.0 us)
Async XLA Ops:
  0.6 286.0 %collective-permute-start = (bf16[1,1024,3584]{2,1,0:T(8,128)(2,1)}, bf16[1,1024,3584]{2,1,0:T(8,128)(2,1)}, u32[]{:S(2)}, u32[]{:S(2)}) collective-permute-start(bf16[1,1024,3584]{2,1,0:T(8,128)(2,1)} %w_ref.1), channel_id=1, source_target_pairs={{0,1},{1,0},{2,3},{3,2},{4,5},{5,4},{6,7},{7,6},{8,9},{9,8},{10,11... | collective-permute-start | bytes 22020104 | tf_op jit(solution)/shard_map/ppermute | solution.py:777
  222.5 1.8 copy-start
  224.4 36.9 %collective-permute-start.2 = (bf16[896,512]{1,0:T(8,128)(2,1)S(1)}, bf16[896,512]{1,0:T(8,128)(2,1)S(1)}, u32[]{:S(2)}, u32[]{:S(2)}) collective-permute-start(bf16[896,512]{1,0:T(8,128)(2,1)S(1)} %constant_dynamic-slice_fusion), channel_id=1, source_target_pairs={{0,1},{1,0},{2,3},{3,2},{4,5},{5,4},{6,7},{7,6},{8,9},{9,8},{10,11... | collective-permute-start | bytes 2752520 | tf_op jit(solution)/shard_map/ppermute | solution.py:793
  225.1 36.3 %collective-permute-start.1 = (bf16[256,512]{1,0:T(8,128)(2,1)S(1)}, bf16[256,512]{1,0:T(8,128)(2,1)S(1)}, u32[]{:S(2)}, u32[]{:S(2)}) collective-permute-start(bf16[256,512]{1,0:T(8,128)(2,1)S(1)} %constant_dynamic-slice_fusion.1), channel_id=1, source_target_pairs={{0,1},{1,0},{2,3},{3,2},{4,5},{5,4},{6,7},{7,6},{8,9},{9,8},{10,11... | collective-permute-start | bytes 786440 | tf_op jit(solution)/shard_map/ppermute | solution.py:791
  226.6 16.4 %copy-start.1 = (bf16[3584,512]{1,0:T(8,128)(2,1)S(1)}, bf16[3584,512]{1,0:T(8,128)(2,1)}, u32[]{:S(2)}) copy-start(bf16[3584,512]{1,0:T(8,128)(2,1)} %copy-done) | copy-start | bytes 11010052
  226.6 60.0 %collective-permute-start.3 = (f32[1,512]{1,0:T(1,128)S(1)}, f32[1,512]{1,0:T(1,128)S(1)}, u32[]{:S(2)}, u32[]{:S(2)}) collective-permute-start(f32[1,512]{1,0:T(1,128)S(1)} %get-tuple-element.11.inv_ref), channel_id=1, source_target_pairs={{0,1},{1,0},{2,3},{3,2},{4,5},{5,4},{6,7},{7,6},{8,9},{9,8},{10,11... | collective-permute-start | bytes 6152 | tf_op jit(solution)/shard_map/ppermute | solution.py:794
  247.1 2.0 copy-start.2
  249.1 3.1 %copy-start.3 = (bf16[1,1024,3584]{2,1,0:T(8,128)(2,1)S(1)}, bf16[1,1024,3584]{2,1,0:T(8,128)(2,1)}, u32[]{:S(2)}) copy-start(bf16[1,1024,3584]{2,1,0:T(8,128)(2,1)} %w_ref.1) | copy-start | bytes 22020100

commit v2 on v1

--- a/solution.py
+++ b/solution.py
@@ -33,7 +33,7 @@
     )
 
 
-def greet(nf, nt):
+def greet(nf, nt, across=False):
     f, t = lax.axis_index("fsdp"), lax.axis_index("tp")
     barrier = pltpu.get_barrier_semaphore()
     n = nf * nt
@@ -47,7 +47,11 @@
         return carry
 
     lax.fori_loop(0, n - 1, one, 0)
-    pl.semaphore_wait(barrier, n - 1)
+    if across:
+        pl.semaphore_signal(
+            barrier, inc=1, device_id={"rollout": 1 - lax.axis_index("rollout")}, device_id_type=MESH
+        )
+    pl.semaphore_wait(barrier, n - 1 + across)
 
 
 def factor_block(s_ref, v_ref):
@@ -122,8 +126,8 @@
 
 
 def mid_kernel(
-    nf, nt, cuts, part_ref, ortho_ref,
-    left, rbuf, lbuf, gpart, gmate, pieces, gram, inverse, work, s_ref, v_ref,
+    nf, nt, cuts, moment_ref, grad_ref, basis_ref, ortho_ref,
+    part_ref, high, low, basis_stage, moment_stage, grad_stage, in_sem, left, rbuf, lbuf, gpart, gmate, pieces, gram, inverse, work, s_ref, v_ref,
     rs_send, rs_recv, mate_send, mate_recv, p_send, p_recv, q_send, q_recv, ag_send, ag_recv,
 ):
     f, t = lax.axis_index("fsdp"), lax.axis_index("tp")
@@ -133,6 +137,30 @@
     share = rows // nt
     sub = share // cuts
     half = rank // 2
+    bits = basis_stage.shape[1]
+    pieces_of_basis = high.shape[0] // bits
+    f32, b16 = jnp.float32, jnp.bfloat16
+
+    def block_at(i):
+        k = jnp.where(lax.rem(i, 2) == 0, nt - 1 - i // 2, i // 2)
+        return jnp.where(t < (nt + 1) // 2, k, nt - 1 - k)
+
+    def fetch_rows(i):
+        where = pl.ds(pl.multiple_of(block_at(i) * share, share), share)
+        slot = lax.rem(i, 2)
+        return (
+            pltpu.make_async_copy(moment_ref.at[0, where], moment_stage.at[slot], in_sem.at[slot]),
+            pltpu.make_async_copy(grad_ref.at[0, where], grad_stage.at[slot], in_sem.at[2 + slot]),
+        )
+
+    def fetch_basis(i):
+        where = pl.ds(pl.multiple_of(i * bits, bits), bits)
+        slot = lax.rem(i, 2)
+        return pltpu.make_async_copy(basis_ref.at[0, where], basis_stage.at[slot], in_sem.at[4 + slot])
+
+    fetch_basis(0).start()
+    for copy in fetch_rows(0):
+        copy.start()
     group = (nf // 2) * nt
     owners = min(group, half // 8)
     piece = half // owners
@@ -154,16 +182,60 @@
     def to_left(src, e, c):
         return remote(src, lbuf.at[e, c], rs_send.at[1, e, c], rs_recv.at[1, e, c], tp=t - 1)
 
+    def split_basis(i, carry):
+        fetch_basis(i).wait()
+
+        @pl.when(i + 1 < pieces_of_basis)
+        def _():
+            fetch_basis(i + 1).start()
+
+        value = basis_stage[lax.rem(i, 2)]
+        where = pl.ds(pl.multiple_of(i * bits, bits), bits)
+        top = value.astype(b16)
+        high[where, :] = top
+        low[where, :] = (value - top.astype(f32)).astype(b16)
+        return carry
+
+    lax.fori_loop(0, pieces_of_basis, split_basis, 0)
+
+    def left_block(i, carry):
+        slot = lax.rem(i, 2)
+        for copy in fetch_rows(i):
+            copy.wait()
+
+        @pl.when(i + 1 < nt)
+        def _():
+            for copy in fetch_rows(i + 1):
+                copy.start()
+
+        d = block_at(i)
+        value = moment_stage[slot] + grad_stage[slot].astype(f32)
+        top = value.astype(b16)
+        rest = (value - top.astype(f32)).astype(b16)
+        part_ref[pl.ds(pl.multiple_of(d * share, share), share), :] = (
+            jnp.dot(top, low[...], preferred_element_type=f32)
+            + jnp.dot(rest, high[...], preferred_element_type=f32)
+            + jnp.dot(top, high[...], preferred_element_type=f32)
+        )
+
+        def begin(c, inner):
+            @pl.when(jnp.logical_and(t == 0, d > 0))
+            def _():
+                to_right(chunk(d, c), d, c).start()
+
+            @pl.when(jnp.logical_and(t == nt - 1, d < nt - 1))
+            def _():
+                to_left(chunk(d, c), d, c).start()
+
+            return inner
+
+        lax.fori_loop(0, cuts, begin, 0)
+        return carry
+
+    lax.fori_loop(0, nt, left_block, 0)
+
     def scatter(i, carry):
         d, e, c = moves(i)
-
-        @pl.when(jnp.logical_and(t < d, t == 0))
-        def _():
-            to_right(chunk(d, c), d, c).start()
-
-        @pl.when(jnp.logical_and(t > e, t == nt - 1))
-        def _():
-            to_left(chunk(e, c), e, c).start()
 
         @pl.when(jnp.logical_and(t < d, t > 0))
         def _():
@@ -263,9 +335,22 @@
     other = remote(gram.at[keep], gram.at[keep], mate_send.at[1], mate_recv.at[1], fsdp=mate)
     other.start()
 
+    def near(q):
+        return jnp.logical_or(q == t + 1, q == t - 1)
+
+    def give_left(q):
+        return remote(left.at[here], left.at[here], ag_send.at[q], ag_recv.at[t], tp=q)
+
+    def give_ortho(q):
+        return remote(ortho_ref.at[here], ortho_ref.at[here], ag_send.at[q], ag_recv.at[t], tp=q)
+
     def gather(i, carry):
         q = lax.rem(t + 1 + i, nt)
-        remote(left.at[here], left.at[here], ag_send.at[q], ag_recv.at[t], tp=q).start()
+
+        @pl.when(near(q))
+        def _():
+            give_left(q).start()
+
         return carry
 
     lax.fori_loop(0, nt - 1, gather, 0)
@@ -274,15 +359,42 @@
     gpart[...] = gram[...]
     factor(gpart, inverse, work, s_ref, v_ref)
 
+    inv_high = inverse[...].astype(b16)
+    inv_low = (inverse[...] - inv_high.astype(f32)).astype(b16)
+
     def ortho_of(i, carry):
         q = lax.rem(t + i, nt)
         there = pl.ds(pl.multiple_of(q * share, share), share)
 
-        @pl.when(i > 0)
+        @pl.when(near(q))
         def _():
             remote(left.at[there], left.at[there], ag_send.at[0], ag_recv.at[q], tp=q).wait_recv()
 
-        ortho_ref[there, :] = dot_t(left[there, :], inverse[...]).astype(jnp.bfloat16)
+        @pl.when(jnp.logical_or(i == 0, near(q)))
+        def _():
+            value = left[there, :]
+            top = value.astype(b16)
+            rest = (value - top.astype(f32)).astype(b16)
+            dims = (((1,), (1,)), ((), ()))
+            ortho_ref[there, :] = (
+                lax.dot_general(top, inv_low, dims, preferred_element_type=f32)
+                + lax.dot_general(rest, inv_high, dims, preferred_element_type=f32)
+                + lax.dot_general(top, inv_high, dims, preferred_element_type=f32)
+            ).astype(b16)
+
+        @pl.when(i == 0)
+        def _():
+            def far_away(k, inner):
+                to = lax.rem(t + 1 + k, nt)
+
+                @pl.when(jnp.logical_not(near(to)))
+                def _():
+                    give_ortho(to).start()
+
+                return inner
+
+            lax.fori_loop(0, nt - 1, far_away, 0)
+
         return carry
 
     lax.fori_loop(0, nt, ortho_of, 0)
@@ -320,28 +432,48 @@
 
     def drain_gather(i, carry):
         q = lax.rem(t + 1 + i, nt)
-        remote(left.at[here], left.at[here], ag_send.at[q], ag_recv.at[t], tp=q).wait_send()
+        there = pl.ds(pl.multiple_of(q * share, share), share)
+
+        @pl.when(near(q))
+        def _():
+            give_left(q).wait_send()
+
+        @pl.when(jnp.logical_not(near(q)))
+        def _():
+            remote(ortho_ref.at[there], ortho_ref.at[there], ag_send.at[0], ag_recv.at[q], tp=q).wait_recv()
+            give_ortho(q).wait_send()
+
         return carry
 
     lax.fori_loop(0, nt - 1, drain_gather, 0)
 
 
-def mid(part, nf, nt):
-    rows, rank = part.shape
+def mid(moment, grad, basis, nf, nt):
+    _, rows, cols = moment.shape
+    rank = basis.shape[2]
     share = rows // nt
-    cuts = 2 if (share // 2) % 8 == 0 else 1
+    cuts = pick(share // 8, (4, 2, 1)) if share % 32 else 4
     sub = share // cuts
     half = rank // 2
     group = (nf // 2) * nt
     owners = min(group, half // 8)
-    f32 = jnp.float32
+    bits = pick(cols, (512, 256, 128))
+    f32, b16 = jnp.float32, jnp.bfloat16
     dma = pltpu.SemaphoreType.DMA
+    hbm = pl.BlockSpec(memory_space=pl.ANY)
     return pl.pallas_call(
         functools.partial(mid_kernel, nf, nt, cuts),
-        out_shape=jax.ShapeDtypeStruct((rows, rank), jnp.bfloat16),
-        in_specs=[pl.BlockSpec(memory_space=pltpu.VMEM)],
+        out_shape=jax.ShapeDtypeStruct((rows, rank), b16),
+        in_specs=[hbm, hbm, hbm],
         out_specs=pl.BlockSpec(memory_space=pltpu.VMEM),
         scratch_shapes=[
+            pltpu.VMEM((rows, rank), f32),
+            pltpu.VMEM((cols, rank), b16),
+            pltpu.VMEM((cols, rank), b16),
+            pltpu.VMEM((2, bits, rank), f32),
+            pltpu.VMEM((2, share, cols), f32),
+            pltpu.VMEM((2, share, cols), b16),
+            dma((6,)),
             pltpu.VMEM((rows, rank), f32),
             pltpu.VMEM((nt, cuts, sub, rank), f32),
             pltpu.VMEM((nt, cuts, sub, rank), f32),
@@ -360,19 +492,20 @@
             dma((nt,)), dma((nt,)),
         ],
         compiler_params=pltpu.CompilerParams(
-            vmem_limit_bytes=40 << 20, collective_id=0, has_side_effects=True
+            vmem_limit_bytes=56 << 20, collective_id=0, has_side_effects=True
         ),
         cost_estimate=pl.CostEstimate(
-            flops=30_000_000_000, bytes_accessed=8 * rank * rank, transcendentals=0
+            flops=60_000_000_000, bytes_accessed=8 * rows * cols, transcendentals=0
         ),
         name="mid",
-    )(part)
+    )(moment, grad, basis)
 
 
 def right_kernel(
-    nf, nt, cuts, cols, part_ref, right_ref, inv_ref,
+    nf, nt, cuts, cols, part_ref, ortho_ref, right_ref, inv_ref, far_ortho, far_right, far_inv,
     mbuf, sbuf, ybuf, sqs,
     m_send, m_recv, y_send, y_recv, g_send, g_recv, w_send, w_recv, sq_send, sq_recv,
+    x_send, x_recv, o_send, o_recv,
 ):
     f, t = lax.axis_index("fsdp"), lax.axis_index("tp")
     core = lax.rem(f, 2)
@@ -386,7 +519,23 @@
     me = f * nt + t
     f32, b16 = jnp.float32, jnp.bfloat16
 
-    greet(nf, nt)
+    far = 1 - lax.axis_index("rollout")
+    share = far_ortho.shape[0] // nt
+
+    greet(nf, nt, True)
+
+    def across(src, dst, i):
+        return remote(src, dst, x_send.at[i], x_recv.at[i], rollout=far)
+
+    def block(q):
+        return pl.ds(pl.multiple_of(q * share, share), share)
+
+    cross_ortho = across(ortho_ref.at[block(t)], far_ortho.at[block(t)], cuts)
+    cross_ortho.start()
+
+    def along(q, source):
+        rows = block(source)
+        return remote(far_ortho.at[rows], far_ortho.at[rows], o_send.at[q], o_recv.at[source], tp=q)
 
     def rows_of(h, q, c):
         return pl.ds(pl.multiple_of(h * half + q * quarter + c * sub, sub), sub)
@@ -425,6 +574,11 @@
         rows = rows_of(core, y, c)
         return remote(
             right_ref.at[rows], right_ref.at[rows], g_send.at[q, c], g_recv.at[y, c], fsdp=2 * q + core
+        )
+
+    def cross_right(c):
+        return across(
+            right_ref.at[rows_of(core, y, c)], far_right.at[pl.ds(pl.multiple_of(c * sub, sub), sub)], c
         )
 
     def to_other_core(q, c):
@@ -451,11 +605,7 @@
         right_ref[rows, :] = total.astype(b16)
         sqs[me] = sqs[me] + jnp.sum((total * total).reshape(sub // 8, 8, total.shape[1]), axis=0)
 
-        def send(i, carry):
-            spread(lax.rem(y + 1 + i, ny), c).start()
-            return carry
-
-        lax.fori_loop(0, ny - 1, send, 0)
+        cross_right(c).start()
         to_other_core(y, c).start()
         return carry
 
@@ -471,6 +621,19 @@
         return carry
 
     lax.fori_loop(0, n - 1, start_squares, 0)
+
+    def start_spread(i, carry):
+        spread(*order(i)).start()
+        return carry
+
+    lax.fori_loop(0, (ny - 1) * cuts, start_spread, 0)
+    cross_ortho.wait_recv()
+
+    def start_along(i, carry):
+        along(lax.rem(t + 1 + i, nt), t).start()
+        return carry
+
+    lax.fori_loop(0, nt - 1, start_along, 0)
 
     def forward(i, carry):
         q, c = order(i)
@@ -493,7 +656,9 @@
     lax.fori_loop(0, n - 1, got_square, 0)
     total = lax.fori_loop(1, n, lambda q, acc: acc + sqs[q], sqs[0])
     meansq = jnp.sum(total, axis=0, keepdims=True) / cols
-    inv_ref[...] = lax.rsqrt(meansq + 1e-06)
+    inv_ref[...] = jnp.broadcast_to(lax.rsqrt(meansq + 1e-06), inv_ref.shape)
+    cross_inv = across(inv_ref, far_inv, cuts + 1)
+    cross_inv.start()
 
     def finish(i, carry):
         q, c = order(i)
@@ -519,6 +684,22 @@
 
     lax.fori_loop(0, n - 1, drain_squares, 0)
 
+    def finish_cross(c, carry):
+        cross_right(c).wait()
+        return carry
+
+    lax.fori_loop(0, cuts, finish_cross, 0)
+    cross_ortho.wait_send()
+    cross_inv.wait()
+
+    def finish_along(i, carry):
+        q = lax.rem(t + 1 + i, nt)
+        along(q, q).wait_recv()
+        along(q, t).wait_send()
+        return carry
+
+    lax.fori_loop(0, nt - 1, finish_along, 0)
+
 
 def sub_blocks(quarter):
     for cuts in (4, 2):
@@ -527,33 +708,39 @@
     return 1
 
 
-def right_sum(part, nf, nt, cols):
+def right_sum(part, ortho, nf, nt, cols):
     mine, rank = part.shape
     ny = nf // 2
     quarter = mine // nf
     cuts = sub_blocks(quarter)
     sub = quarter // cuts
     n = nf * nt
-    b16 = jnp.bfloat16
+    b16, f32 = jnp.bfloat16, jnp.float32
     dma = pltpu.SemaphoreType.DMA
+    vmem = pl.BlockSpec(memory_space=pltpu.VMEM)
     return pl.pallas_call(
         functools.partial(right_kernel, nf, nt, cuts, cols),
         out_shape=(
             jax.ShapeDtypeStruct((mine, rank), b16),
-            jax.ShapeDtypeStruct((1, rank), jnp.float32),
-        ),
-        in_specs=[pl.BlockSpec(memory_space=pltpu.VMEM)],
-        out_specs=(pl.BlockSpec(memory_space=pltpu.VMEM), pl.BlockSpec(memory_space=pltpu.VMEM)),
+            jax.ShapeDtypeStruct((8, rank), f32),
+            jax.ShapeDtypeStruct(ortho.shape, b16),
+            jax.ShapeDtypeStruct((quarter, rank), b16),
+            jax.ShapeDtypeStruct((8, rank), f32),
+        ),
+        in_specs=[vmem, vmem],
+        out_specs=(vmem,) * 5,
         scratch_shapes=[
             pltpu.VMEM((ny, cuts, sub, rank), b16),
             pltpu.VMEM((ny, cuts, sub, rank), b16),
             pltpu.VMEM((ny, cuts, sub, rank), b16),
-            pltpu.VMEM((n, 8, rank), jnp.float32),
+            pltpu.VMEM((n, 8, rank), f32),
             dma((ny, cuts)), dma((ny, cuts)),
             dma((ny, cuts)), dma((ny, cuts)),
             dma((ny, cuts)), dma((ny, cuts)),
             dma((ny, cuts)), dma((ny, cuts)),
             dma((n,)), dma((n,)),
+            dma((cuts + 2,)), dma((cuts + 2,)),
+            dma((nt,)), dma((nt,)),
         ],
         compiler_params=pltpu.CompilerParams(
             vmem_limit_bytes=40 << 20, collective_id=1, has_side_effects=True
@@ -562,244 +749,155 @@
             flops=10_000_000_000, bytes_accessed=4 * mine * rank, transcendentals=0
         ),
         name="right_sum",
-    )(part)
-
-
-def spread_kernel(
-    nf, nt, cuts, o_ref, r_ref, ortho_ref, right_ref,
-    o_send, o_recv, g_send, g_recv, w_send, w_recv, here_sem,
+    )(part, ortho)
+
+
+def own_kernel(
+    who_ref, w_ref, g_ref, m_ref, ortho_ref, right_ref, inv_ref, new_ref, both_ref, moment_ref, basis_ref
 ):
-    f, t = lax.axis_index("fsdp"), lax.axis_index("tp")
-    core = lax.rem(f, 2)
-    y = f // 2
-    ny = nf // 2
-    mate = f + 1 - 2 * core
-    share = o_ref.shape[0]
-    quarter = r_ref.shape[0]
-    half = quarter * ny
-    sub = quarter // cuts
-
-    greet(nf, nt)
-
-    def rows_of(h, q, c):
-        return pl.ds(pl.multiple_of(h * half + q * quarter + c * sub, sub), sub)
-
-    def mine(c):
-        return r_ref.at[pl.ds(pl.multiple_of(c * sub, sub), sub)]
-
-    def block(q):
-        return pl.ds(pl.multiple_of(q * share, share), share)
-
-    def order(i):
-        return lax.rem(y + 1 + i // cuts, ny), lax.rem(i, cuts)
-
-    def to_peer(q, c):
-        return remote(
-            mine(c), right_ref.at[rows_of(core, y, c)], g_send.at[q, c], g_recv.at[y, c],
-            fsdp=2 * q + core,
-        )
-
-    def start_peer(i, carry):
-        q, c = order(i)
-        to_peer(q, c).start()
-        return carry
-
-    lax.fori_loop(0, (ny - 1) * cuts, start_peer, 0)
-
-    def to_line(q):
-        return remote(o_ref, ortho_ref.at[block(t)], o_send.at[q], o_recv.at[t], tp=q)
-
-    def start_line(i, carry):
-        to_line(lax.rem(t + 1 + i, nt)).start()
-        return carry
-
-    lax.fori_loop(0, nt - 1, start_line, 0)
-
-    def own_to_mate(c):
-        return remote(
-            mine(c), right_ref.at[rows_of(core, y, c)], w_send.at[y, c], w_recv.at[y, c], fsdp=mate
-        )
-
-    def start_own(c, carry):
-        own_to_mate(c).start()
-        return carry
-
-    lax.fori_loop(0, cuts, start_own, 0)
-    first = pltpu.make_async_copy(o_ref, ortho_ref.at[block(t)], here_sem.at[0])
-    second = pltpu.make_async_copy(
-        r_ref, right_ref.at[pl.ds(pl.multiple_of(core * half + y * quarter, quarter), quarter)], here_sem.at[1]
-    )
-    first.start()
-    second.start()
-
-    def to_other_core(q, c):
-        rows = rows_of(core, q, c)
-        return remote(
-            right_ref.at[rows], right_ref.at[rows], w_send.at[q, c], w_recv.at[q, c], fsdp=mate
-        )
-
-    def forward(i, carry):
-        q, c = order(i)
-        rows = rows_of(core, q, c)
-        remote(mine(c), right_ref.at[rows], g_send.at[q, c], g_recv.at[q, c], fsdp=2 * q + core).wait_recv()
-        to_other_core(q, c).start()
-        return carry
-
-    lax.fori_loop(0, (ny - 1) * cuts, forward, 0)
-
-    def finish(i, carry):
-        q, c = order(i)
-        rows = rows_of(1 - core, q, c)
-        remote(
-            right_ref.at[rows], right_ref.at[rows], w_send.at[q, c], w_recv.at[q, c], fsdp=mate
-        ).wait_recv()
-        to_other_core(q, c).wait_send()
-
-        @pl.when(q != y)
-        def _():
-            to_peer(q, c).wait_send()
-
-        return carry
-
-    lax.fori_loop(0, ny * cuts, finish, 0)
-
-    def finish_line(i, carry):
-        q = lax.rem(t + 1 + i, nt)
-        remote(o_ref, ortho_ref.at[block(q)], o_send.at[q], o_recv.at[q], tp=q).wait_recv()
-        to_line(q).wait_send()
-        return carry
-
-    lax.fori_loop(0, nt - 1, finish_line, 0)
-    first.wait()
-    second.wait()
-
-
-def spread_other(ortho, right, nf, nt):
-    share, rank = ortho.shape
-    quarter = right.shape[0]
-    ny = nf // 2
-    cuts = sub_blocks(quarter)
-    dma = pltpu.SemaphoreType.DMA
-    vmem = pl.BlockSpec(memory_space=pltpu.VMEM)
-    return pl.pallas_call(
-        functools.partial(spread_kernel, nf, nt, cuts),
-        out_shape=(
-            jax.ShapeDtypeStruct((share * nt, rank), jnp.bfloat16),
-            jax.ShapeDtypeStruct((quarter * nf, rank), jnp.bfloat16),
-        ),
-        in_specs=[vmem, vmem],
-        out_specs=(vmem, vmem),
-        scratch_shapes=[
-            dma((nt,)), dma((nt,)),
-            dma((ny, cuts)), dma((ny, cuts)),
-            dma((ny, cuts)), dma((ny, cuts)),
-            dma((2,)),
-        ],
-        compiler_params=pltpu.CompilerParams(
-            vmem_limit_bytes=32 << 20, collective_id=2, has_side_effects=True
-        ),
-        cost_estimate=pl.CostEstimate(
-            flops=5_000_000_000, bytes_accessed=4 * quarter * nf * rank, transcendentals=0
-        ),
-        name="spread_other",
-    )(ortho, right)
-
-
-def updated(w_ref, ortho_ref, right_ref, inv_ref):
-    base = (right_ref[...].astype(jnp.float32) * inv_ref[...]).astype(jnp.bfloat16)
-    update = lax.dot_general(
-        ortho_ref[...], base, (((1,), (1,)), ((), ())), preferred_element_type=jnp.float32
-    )
-    return (w_ref[0].astype(jnp.float32) - 0.3 * update).astype(jnp.bfloat16)
-
-
-def own_kernel(who_ref, w_ref, ortho_ref, right_ref, inv_ref, new_ref, both_ref):
-    value = updated(w_ref, ortho_ref, right_ref, inv_ref)
+    f32 = jnp.float32
+    dims = (((1,), (1,)), ((), ()))
+    tc = w_ref.shape[2]
+    right = right_ref[pl.ds(pl.multiple_of(pl.program_id(0) * tc, tc), tc), :]
+    ortho = ortho_ref[...]
+    basis = right.astype(f32) * inv_ref[0:1, :]
+    basis_ref[0] = basis
+    update = lax.dot_general(ortho, basis.astype(jnp.bfloat16), dims, preferred_element_type=f32)
+    value = (w_ref[0].astype(f32) - 0.3 * update).astype(jnp.bfloat16)
     new_ref[0] = value
     both_ref[0] = value
-
-
-def other_kernel(who_ref, w_ref, ortho_ref, right_ref, inv_ref, both_in, both_ref):
-    both_ref[0] = updated(w_ref, ortho_ref, right_ref, inv_ref)
-
-
-def apply_update(who, w, ortho, right, inv, both=None):
+    blend = m_ref[0] + g_ref[0].astype(f32)
+    moment_ref[0] = blend - 0.05 * lax.dot_general(ortho, right, dims, preferred_element_type=f32)
+
+
+def apply_own(who, w, g, m, ortho, right, inv):
     _, rows, cols = w.shape
     rank = ortho.shape[1]
-    tr = pick(rows, (512, 256, 128))
-    tc = pick(cols, (896, 512, 256, 128))
-    w_spec = pl.BlockSpec((1, tr, tc), lambda j, i, who: (0, i, j))
-    both_spec = pl.BlockSpec((1, tr, tc), lambda j, i, who: (who[0], i, j))
-    in_specs = [
-        w_spec,
-        pl.BlockSpec((tr, rank), lambda j, i, who: (i, 0)),
-        pl.BlockSpec((tc, rank), lambda j, i, who: (j, 0)),
-        pl.BlockSpec((1, rank), lambda j, i, who: (0, 0)),
-    ]
-    both_shape = jax.ShapeDtypeStruct((2, rows, cols), jnp.bfloat16)
-    args = [who, w, ortho, right, inv]
-    if both is None:
-        kernel = own_kernel
-        out_shape = (jax.ShapeDtypeStruct((1, rows, cols), jnp.bfloat16), both_shape)
-        out_specs = (w_spec, both_spec)
-        aliases = {}
-    else:
-        kernel = other_kernel
-        in_specs.append(pl.BlockSpec(memory_space=pl.ANY))
-        args.append(both)
-        out_shape = both_shape
-        out_specs = both_spec
-        aliases = {5: 0}
+    tc = pick(cols, (512, 256, 128))
+    spec = pl.BlockSpec((1, rows, tc), lambda j, who: (0, 0, j))
+    f32, b16 = jnp.float32, jnp.bfloat16
     return pl.pallas_call(
-        kernel,
-        out_shape=out_shape,
+        own_kernel,
+        out_shape=(
+            jax.ShapeDtypeStruct((1, rows, cols), b16),
+            jax.ShapeDtypeStruct((2, rows, cols), b16),
+            jax.ShapeDtypeStruct((1, rows, cols), f32),
+            jax.ShapeDtypeStruct((1, cols, rank), f32),
+        ),
         grid_spec=pltpu.PrefetchScalarGridSpec(
             num_scalar_prefetch=1,
-            grid=(cols // tc, rows // tr),
-            in_specs=in_specs,
-            out_specs=out_specs,
-        ),
-        input_output_aliases=aliases,
-        compiler_params=pltpu.CompilerParams(vmem_limit_bytes=32 << 20),
+            grid=(cols // tc,),
+            in_specs=[
+                spec,
+                spec,
+                spec,
+                pl.BlockSpec(memory_space=pltpu.VMEM),
+                pl.BlockSpec(memory_space=pltpu.VMEM),
+                pl.BlockSpec(memory_space=pltpu.VMEM),
+            ],
+            out_specs=(
+                spec,
+                pl.BlockSpec((1, rows, tc), lambda j, who: (who[0], 0, j)),
+                spec,
+                pl.BlockSpec((1, tc, rank), lambda j, who: (0, j, 0)),
+            ),
+        ),
+        compiler_params=pltpu.CompilerParams(vmem_limit_bytes=48 << 20),
         cost_estimate=pl.CostEstimate(
-            flops=2 * rows * cols * rank, bytes_accessed=6 * rows * cols, transcendentals=0
-        ),
-        name="apply_own" if both is None else "apply_other",
-    )(*args)
+            flops=30_000_000_000, bytes_accessed=18 * rows * cols, transcendentals=0
+        ),
+        name="apply_own",
+    )(who, w, g, m, ortho, right, inv)
+
+
+def other_kernel(nf, who_ref, *refs):
+    rights = refs[:nf]
+    ortho, w_ref, inv_ref, _, both_ref, base = refs[nf:]
+    quarter = rights[0].shape[0]
+    f32, b16 = jnp.float32, jnp.bfloat16
+    j = pl.program_id(0)
+
+    @pl.when(j == 0)
+    def _():
+        inv = inv_ref[0:1, :]
+        for k, piece in enumerate(rights):
+            place = pl.ds(pl.multiple_of(who_ref[1 + k] * quarter, quarter), quarter)
+            base[place, :] = (piece[...].astype(f32) * inv).astype(b16)
+
+    tc = w_ref.shape[2]
+    update = lax.dot_general(
+        ortho[...],
+        base[pl.ds(pl.multiple_of(j * tc, tc), tc), :],
+        (((1,), (1,)), ((), ())),
+        preferred_element_type=f32,
+    )
+    both_ref[0] = (w_ref[0].astype(f32) - 0.3 * update).astype(b16)
+
+
+def apply_other(who, rights, ortho, w, inv, both):
+    _, rows, cols = w.shape
+    rank = inv.shape[1]
+    nf = len(rights)
+    tc = pick(cols, (512, 256, 128))
+    whole = pl.BlockSpec(memory_space=pltpu.VMEM)
+    return pl.pallas_call(
+        functools.partial(other_kernel, nf),
+        out_shape=jax.ShapeDtypeStruct((2, rows, cols), jnp.bfloat16),
+        grid_spec=pltpu.PrefetchScalarGridSpec(
+            num_scalar_prefetch=1,
+            grid=(cols // tc,),
+            in_specs=[whole] * (nf + 1)
+            + [
+                pl.BlockSpec((1, rows, tc), lambda j, who: (0, 0, j)),
+                whole,
+                pl.BlockSpec(memory_space=pl.ANY),
+            ],
+            out_specs=pl.BlockSpec((1, rows, tc), lambda j, who: (who[0], 0, j)),
+            scratch_shapes=[pltpu.VMEM((cols, rank), jnp.bfloat16)],
+        ),
+        input_output_aliases={nf + 4: 0},
+        compiler_params=pltpu.CompilerParams(vmem_limit_bytes=40 << 20),
+        cost_estimate=pl.CostEstimate(
+            flops=2 * rows * cols * rank, bytes_accessed=4 * rows * cols, transcendentals=0
+        ),
+        name="apply_other",
+    )(who, *rights, ortho, w, inv, both)
 
 
 def body(weights, gradient, momentum, basis):
     swap = functools.partial(lax.ppermute, axis_name="rollout", perm=[(0, 1), (1, 0)])
     me = lax.axis_index("rollout")
-    f, t = lax.axis_index("fsdp"), lax.axis_index("tp")
+    f = lax.axis_index("fsdp")
     nf, nt = lax.axis_size("fsdp"), lax.axis_size("tp")
     cols = weights.shape[2] * nt
     weights_other = swap(weights)
     blend = momentum[0] + gradient[0].astype(jnp.float32)
-    part = jnp.dot(blend, basis[0], precision=HIGH, preferred_element_type=jnp.float32)
-    ortho = mid(part, nf, nt)
-    rows = ortho.shape[0]
+    ortho = mid(momentum, gradient, basis, nf, nt)
     partial_right = lax.dot_general(
         blend.astype(jnp.bfloat16),
         ortho,
         (((0,), (0,)), ((), ())),
         preferred_element_type=jnp.float32,
     ).astype(jnp.bfloat16)
-    right, inv = right_sum(partial_right, nf, nt, cols)
-    share = rows // nt
-    quarter = right.shape[0] // nf
-    ortho_piece = swap(lax.dynamic_slice_in_dim(ortho, t * share, share, 0))
-    place = (f % 2) * (nf // 2) + f // 2
-    right_piece = swap(lax.dynamic_slice_in_dim(right, place * quarter, quarter, 0))
-    inv_other = swap(inv)
-    weight_new, both = apply_update(me.reshape(1), weights, ortho, right, inv)
-    moment_new = blend - 0.05 * lax.dot_general(
-        ortho, right, (((1,), (1,)), ((), ())), preferred_element_type=jnp.float32
+    right, inv, far_ortho, far_right, inv_other = right_sum(partial_right, ortho, nf, nt, cols)
+    ny = nf // 2
+    core, y = f % 2, f // 2
+    mates = [(i, i ^ 1) for i in range(nf)]
+    rights, right_places = [far_right], [core * ny + y]
+    for k in range(1, ny):
+        rights.append(
+            lax.ppermute(far_right, "fsdp", [(i, ((i // 2 - k) % ny) * 2 + i % 2) for i in range(nf)])
+        )
+        right_places.append(core * ny + (y + k) % ny)
+    for k in range(ny):
+        rights.append(lax.ppermute(rights[k], "fsdp", mates))
+        right_places.append((1 - core) * ny + (y + k) % ny)
+    weight_new, both, moment_new, basis_new = apply_own(
+        me.reshape(1), weights, gradient, momentum, ortho, right, inv
     )
-    basis_new = right.astype(jnp.float32) * inv
-    ortho_other, right_other = spread_other(ortho_piece, right_piece, nf, nt)
-    both = apply_update((1 - me).reshape(1), weights_other, ortho_other, right_other, inv_other, both)
-    return (weight_new, moment_new[None], basis_new[None], both)
+    who = jnp.stack([1 - me] + right_places).astype(jnp.int32)
+    both = apply_other(who, rights, far_ortho, weights_other, inv_other, both)
+    return (weight_new, moment_new, basis_new, both)
 
 
 def solution(mesh):

time: 298 us -> 274 us (0.919)
  matrix products: 57.3 us -> 11.6 us
  waiting for transfers between devices: 0.01 us -> 20.5 us
  Pallas kernels: 223 us -> 230 us
  other arithmetic: 4.1 us -> 0 us
    dot_general x2 -> x0, matrix products: 44.1 us -> none  [the longest x1 28.3 us: body(): jnp.dot(blend, basis[0], precision=HIGH, preferred_element_type=jnp.float32)]
    pallas_call x1, Pallas kernels: 114 us -> 139 us  [mid(): pl.pallas_call(functools.partial(mid_kernel, nf, nt, cuts), out_shape=jax...]
    ppermute x3, waiting for transfers between devices: 0.01 us -> 20.5 us  [the longest x1 20.5 us: body(): lax.ppermute(far_right, 'fsdp', [(i, (i // 2 - k) % ny * 2 + i % 2) for i...]
    pallas_call x1, Pallas kernels: 63 us -> 54 us  [right_sum(): pl.pallas_call(functools.partial(right_kernel, nf, nt, cuts, cols), out_s...]
    pallas_call x3 -> x2, Pallas kernels: 45.2 us -> 37 us  [the longest x1 25.2 us: apply_own(): pl.pallas_call(own_kernel, out_shape=(jax.ShapeDtypeStruct((1, rows, cols...]
    broadcast_in_dim x1 -> x0, other arithmetic: 4.1 us -> none  [body(): return (weight_new, moment_new[None], basis_new[None], both)]
  transfers between devices with their start and end apart: 4 -> 4, of which waited for: 0 -> 1; matrix products, arithmetic and copies ran while one was open for 21% -> 4% of each run, Pallas kernels for 71% -> 80%
where the time goes in v2:
time: 274 us; the launch traced here: 272 us
  Pallas kernels  230 us (84%)
  waiting for transfers between devices  20.5 us (7%)
  matrix products  11.6 us (4%)
  local copies, waits for them, and re-layouts  5.18 us (2%)
  starting transfers between devices  4.15 us (2%)
    pallas_call x1, Pallas kernels, mid(): pl.pallas_call(functools.partial(mid_kernel, nf, nt, cuts), out_shape=jax...  139 us
    pallas_call x1, Pallas kernels, right_sum(): pl.pallas_call(functools.partial(right_kernel, nf, nt, cuts, cols), out_s...  54 us
    pallas_call x1, Pallas kernels, apply_own(): pl.pallas_call(own_kernel, out_shape=(jax.ShapeDtypeStruct((1, rows, cols...  25.2 us
    ppermute x1, waiting for transfers between devices, body(): lax.ppermute(far_right, 'fsdp', [(i, (i // 2 - k) % ny * 2 + i % 2) for i...  20.5 us
    pallas_call x1, Pallas kernels, apply_other(): pl.pallas_call(functools.partial(other_kernel, nf), out_shape=jax.ShapeDt...  11.8 us
    dot_general x1, matrix products, body(): lax.dot_general(blend.astype(jnp.bfloat16), ortho, (((0,), (0,)), ((), ()...  11.6 us
  transfers between devices with their start and end apart: 4, of which 1 were waited for; matrix products, arithmetic and copies ran while one was open for 4% of the time, Pallas kernels for 80%

profile of v2, /device:TPU:0, one launch (start us, length us, event | category | flops | bytes accessed | tf_op | source)
XLA Modules:
  0.0 272.3 jit_solution(504365999790912592)
XLA Ops:
  0.6 3.0 %collective-permute-start.3 = (bf16[1,1024,3584]{2,1,0:T(8,128)(2,1)}, bf16[1,1024,3584]{2,1,0:T(8,128)(2,1)}, u32[]{:S(2)}, u32[]{:S(2)}) collective-permute-start(bf16[1,1024,3584]{2,1,0:T(8,128)(2,1)} %w_ref.1), channel_id=1, source_target_pairs={{0,1},{1,0},{2,3},{3,2},{4,5},{5,4},{6,7},{7,6},{8,9},{9,8},{10,11... | collective-permute-start | bytes 22020104 | tf_op jit(solution)/shard_map/ppermute | solution.py:873
  3.7 139.1 %mid.1.ortho_ref = bf16[1024,512]{1,0:T(8,128)(2,1)} custom-call(f32[1,1024,3584]{2,1,0:T(8,128)} %m_ref.1, bf16[1,1024,3584]{2,1,0:T(8,128)(2,1)} %g_ref.1, f32[1,3584,512]{2,1,0:T(8,128)} %basis_ref.1), custom_call_target="tpu_custom_call" | custom-call | flops 60000002048 | bytes 29360128 | tf_op jit(solution)/shard_map/mid/pallas_call | solution.py:464
  142.8 0.0 copy-start
  142.8 11.6 %fusion.3.part_ref = bf16[3584,512]{1,0:T(8,128)(2,1)S(1)} fusion(bf16[1024,512]{1,0:T(8,128)(2,1)} %mid.1.ortho_ref, f32[1,1024,3584]{2,1,0:T(8,128)} %m_ref.1, bf16[1,1024,3584]{2,1,0:T(8,128)(2,1)} %g_ref.1), kind=kOutput, calls=%fused_computation.3 | convolution fusion | flops 3770941440 | bytes 26738688 | tf_op jit(solution)/shard_map/dot_general | solution.py:876
  154.4 0.0 copy-done
  154.5 54.0 %right_sum.1 = (bf16[3584,512]{1,0:T(8,128)(2,1)S(1)}, f32[8,512]{1,0:T(8,128)S(1)}, bf16[1024,512]{1,0:T(8,128)(2,1)S(1)}, bf16[896,512]{1,0:T(8,128)(2,1)S(1)}, f32[8,512]{1,0:T(8,128)S(1)}) custom-call(bf16[3584,512]{1,0:T(8,128)(2,1)S(1)} %fusion.3.part_ref, bf16[1024,512]{1,0:T(8,128)(2,1)S(1)} %copy-done), custom_call_target="tpu_custom_call" | custom-call | flops 10000000000 | bytes 7340032 | tf_op jit(solution)/shard_map/right_sum/pallas_call | solution.py:721
  208.5 0.0 copy-start.2
  208.5 1.8 copy-done.2
  210.3 1.1 collective-permute-start
  211.4 0.0 collective-permute-start.1
  211.4 20.5 %collective-permute-done.refs_1_ = bf16[896,512]{1,0:T(8,128)(2,1)S(1)} collective-permute-done((bf16[896,512]{1,0:T(8,128)(2,1)S(1)}, bf16[896,512]{1,0:T(8,128)(2,1)S(1)}, u32[]{:S(2)}, u32[]{:S(2)}) %collective-permute-start) | collective-permute-done | bytes 917536 | tf_op jit(solution)/shard_map/ppermute | solution.py:889
  231.9 0.0 collective-permute-start.2
  231.9 0.0 copy-start.1
  231.9 1.2 copy-done.1
  233.2 0.0 copy-start.3
  233.2 2.0 copy-done.3
  235.2 25.2 %apply_own.1 = (bf16[1,1024,3584]{2,1,0:T(8,128)(2,1)}, bf16[2,1024,3584]{2,1,0:T(8,128)(2,1)}, f32[1,1024,3584]{2,1,0:T(8,128)}, f32[1,3584,512]{2,1,0:T(8,128)}) custom-call(s32[1]{0:T(128)} %bitcast.who_ref, bf16[1,1024,3584]{2,1,0:T(8,128)(2,1)} %w_ref.1, bf16[1,1024,3584]{2,1,0:T(8,128)(2,1)} %g_ref.1, f32[1,1024,3584]{2,1,0:T(8,128)} %m_ref.1, ...), custom_call_target="tpu_custom_call" | custom-call | flops 30000001024 | bytes 66060288 | tf_op jit(solution)/shard_map/apply_own/pallas_call | solution.py:779
  260.4 0.1 stack.23.who_ref
  260.5 0.0 collective-permute-done.1.refs_2_
  260.5 0.0 collective-permute-done.2.refs_3_
  260.5 0.0 collective-permute-done.3.refs_5_
  260.5 11.8 %apply_other.1 = bf16[2,1024,3584]{2,1,0:T(8,128)(2,1)} custom-call(s32[5]{0:T(128)S(1)} %stack.23.who_ref, bf16[896,512]{1,0:T(8,128)(2,1)S(1)} %get-tuple-element.18.refs_0_, bf16[896,512]{1,0:T(8,128)(2,1)S(1)} %collective-permute-done.refs_1_, bf16[896,512]{1,0:T(8,128)(2,1)} %collective-permute-done.1.refs_2_, ...), custom_call_target="tpu_custom_call", output_to_operand_aliasing={{}: (8, {})} | custom-call | flops 3758096384 | bytes 14680064 | tf_op jit(solution)/shard_map/apply_other/pallas_call | solution.py:843
Async XLA Ops:
  0.6 259.9 %collective-permute-start.3 = (bf16[1,1024,3584]{2,1,0:T(8,128)(2,1)}, bf16[1,1024,3584]{2,1,0:T(8,128)(2,1)}, u32[]{:S(2)}, u32[]{:S(2)}) collective-permute-start(bf16[1,1024,3584]{2,1,0:T(8,128)(2,1)} %w_ref.1), channel_id=1, source_target_pairs={{0,1},{1,0},{2,3},{3,2},{4,5},{5,4},{6,7},{7,6},{8,9},{9,8},{10,11... | collective-permute-start | bytes 22020104 | tf_op jit(solution)/shard_map/ppermute | solution.py:873
  142.8 11.7 %copy-start = (bf16[1024,512]{1,0:T(8,128)(2,1)S(1)}, bf16[1024,512]{1,0:T(8,128)(2,1)}, u32[]{:S(2)}) copy-start(bf16[1024,512]{1,0:T(8,128)(2,1)} %mid.1.ortho_ref) | copy-start | bytes 3145732
  208.5 1.8 copy-start.2
  210.3 21.6 %collective-permute-start = (bf16[896,512]{1,0:T(8,128)(2,1)S(1)}, bf16[896,512]{1,0:T(8,128)(2,1)S(1)}, u32[]{:S(2)}, u32[]{:S(2)}) collective-permute-start(bf16[896,512]{1,0:T(8,128)(2,1)S(1)} %get-tuple-element.18.refs_0_), channel_id=1, source_target_pairs={{0,16},{8,24},{16,0},{24,8},{1,17},{9,25},{17,1},{25,9},{2,18},{10... | collective-permute-start | bytes 2752520 | tf_op jit(solution)/shard_map/ppermute | solution.py:889
  211.4 49.1 %collective-permute-start.1 = (bf16[896,512]{1,0:T(8,128)(2,1)S(1)}, bf16[896,512]{1,0:T(8,128)(2,1)}, u32[]{:S(2)}, u32[]{:S(2)}) collective-permute-start(bf16[896,512]{1,0:T(8,128)(2,1)S(1)} %get-tuple-element.18.refs_0_), channel_id=1, source_target_pairs={{0,8},{8,0},{16,24},{24,16},{1,9},{9,1},{17,25},{25,17},{2,10},{10... | collective-permute-start | bytes 2752520 | tf_op jit(solution)/shard_map/ppermute | solution.py:893
  231.9 28.6 %collective-permute-start.2 = (bf16[896,512]{1,0:T(8,128)(2,1)S(1)}, bf16[896,512]{1,0:T(8,128)(2,1)}, u32[]{:S(2)}, u32[]{:S(2)}) collective-permute-start(bf16[896,512]{1,0:T(8,128)(2,1)S(1)} %collective-permute-done.refs_1_), channel_id=1, source_target_pairs={{0,8},{8,0},{16,24},{24,16},{1,9},{9,1},{17,25},{25,17},{2,10},{10... | collective-permute-start | bytes 2752520 | tf_op jit(solution)/shard_map/ppermute | solution.py:893
  231.9 1.2 copy-start.1
  233.2 2.0 copy-start.3

commit v3 on v2

--- a/solution.py
+++ b/solution.py
@@ -126,7 +126,7 @@
 
 
 def mid_kernel(
-    nf, nt, cuts, moment_ref, grad_ref, basis_ref, ortho_ref,
+    nf, nt, cuts, moment_ref, grad_ref, basis_ref, ortho_ref, blend_ref,
     part_ref, high, low, basis_stage, moment_stage, grad_stage, in_sem, left, rbuf, lbuf, gpart, gmate, pieces, gram, inverse, work, s_ref, v_ref,
     rs_send, rs_recv, mate_send, mate_recv, p_send, p_recv, q_send, q_recv, ag_send, ag_recv,
 ):
@@ -212,6 +212,7 @@
         value = moment_stage[slot] + grad_stage[slot].astype(f32)
         top = value.astype(b16)
         rest = (value - top.astype(f32)).astype(b16)
+        blend_ref[pl.ds(pl.multiple_of(d * share, share), share), :] = top
         part_ref[pl.ds(pl.multiple_of(d * share, share), share), :] = (
             jnp.dot(top, low[...], preferred_element_type=f32)
             + jnp.dot(rest, high[...], preferred_element_type=f32)
@@ -463,9 +464,12 @@
     hbm = pl.BlockSpec(memory_space=pl.ANY)
     return pl.pallas_call(
         functools.partial(mid_kernel, nf, nt, cuts),
-        out_shape=jax.ShapeDtypeStruct((rows, rank), b16),
+        out_shape=(
+            jax.ShapeDtypeStruct((rows, rank), b16),
+            jax.ShapeDtypeStruct((rows, cols), b16),
+        ),
         in_specs=[hbm, hbm, hbm],
-        out_specs=pl.BlockSpec(memory_space=pltpu.VMEM),
+        out_specs=(pl.BlockSpec(memory_space=pltpu.VMEM),) * 2,
         scratch_shapes=[
             pltpu.VMEM((rows, rank), f32),
             pltpu.VMEM((cols, rank), b16),
@@ -492,7 +496,7 @@
             dma((nt,)), dma((nt,)),
         ],
         compiler_params=pltpu.CompilerParams(
-            vmem_limit_bytes=56 << 20, collective_id=0, has_side_effects=True
+            vmem_limit_bytes=52 << 20, collective_id=0, has_side_effects=True
         ),
         cost_estimate=pl.CostEstimate(
             flops=60_000_000_000, bytes_accessed=8 * rows * cols, transcendentals=0
@@ -871,10 +875,9 @@
     nf, nt = lax.axis_size("fsdp"), lax.axis_size("tp")
     cols = weights.shape[2] * nt
     weights_other = swap(weights)
-    blend = momentum[0] + gradient[0].astype(jnp.float32)
-    ortho = mid(momentum, gradient, basis, nf, nt)
+    ortho, blend = mid(momentum, gradient, basis, nf, nt)
     partial_right = lax.dot_general(
-        blend.astype(jnp.bfloat16),
+        blend,
         ortho,
         (((0,), (0,)), ((), ())),
         preferred_element_type=jnp.float32,

time: 274 us -> 272 us (level)
  matrix products: 11.6 us -> 7.75 us
    dot_general x1, matrix products: 11.6 us -> 7.75 us  [body(): lax.dot_general(blend, ortho, (((0,), (0,)), ((), ())), preferred_element...]
  transfers between devices with their start and end apart: 4 -> 4, of which waited for: 1 -> 1; matrix products, arithmetic and copies ran while one was open for 4% -> 3% of each run, Pallas kernels for 80% -> 81%
where the time goes in v3:
time: 272 us; the launch traced here: 270 us
  Pallas kernels  232 us (85%)
  waiting for transfers between devices  20.6 us (8%)
  matrix products  7.75 us (3%)
  local copies, waits for them, and re-layouts  5.18 us (2%)
  starting transfers between devices  4.09 us (2%)
    pallas_call x1, Pallas kernels, mid(): pl.pallas_call(functools.partial(mid_kernel, nf, nt, cuts), out_shape=(ja...  141 us
    pallas_call x1, Pallas kernels, right_sum(): pl.pallas_call(functools.partial(right_kernel, nf, nt, cuts, cols), out_s...  54 us
    pallas_call x1, Pallas kernels, apply_own(): pl.pallas_call(own_kernel, out_shape=(jax.ShapeDtypeStruct((1, rows, cols...  25.2 us
    ppermute x1, waiting for transfers between devices, body(): lax.ppermute(far_right, 'fsdp', [(i, (i // 2 - k) % ny * 2 + i % 2) for i...  20.6 us
    pallas_call x1, Pallas kernels, apply_other(): pl.pallas_call(functools.partial(other_kernel, nf), out_shape=jax.ShapeDt...  11.8 us
    dot_general x1, matrix products, body(): lax.dot_general(blend, ortho, (((0,), (0,)), ((), ())), preferred_element...  7.75 us
  transfers between devices with their start and end apart: 4, of which 1 were waited for; matrix products, arithmetic and copies ran while one was open for 3% of the time, Pallas kernels for 81%

profile of v3, /device:TPU:0, one launch (start us, length us, event | category | flops | bytes accessed | tf_op | source)
XLA Modules:
  0.0 270.5 jit_solution(7782599735003617889)
XLA Ops:
  0.6 3.0 %collective-permute-start.3 = (bf16[1,1024,3584]{2,1,0:T(8,128)(2,1)}, bf16[1,1024,3584]{2,1,0:T(8,128)(2,1)}, u32[]{:S(2)}, u32[]{:S(2)}) collective-permute-start(bf16[1,1024,3584]{2,1,0:T(8,128)(2,1)} %w_ref.1), channel_id=1, source_target_pairs={{0,1},{1,0},{2,3},{3,2},{4,5},{5,4},{6,7},{7,6},{8,9},{9,8},{10,11... | collective-permute-start | bytes 22020104 | tf_op jit(solution)/shard_map/ppermute | solution.py:877
  3.7 141.1 %mid.1 = (bf16[1024,512]{1,0:T(8,128)(2,1)S(1)}, bf16[1024,3584]{1,0:T(8,128)(2,1)}) custom-call(f32[1,1024,3584]{2,1,0:T(8,128)} %m_ref.1, bf16[1,1024,3584]{2,1,0:T(8,128)(2,1)} %g_ref.1, f32[1,3584,512]{2,1,0:T(8,128)} %basis_ref.1), custom_call_target="tpu_custom_call" | custom-call | flops 60000002048 | bytes 29360128 | tf_op jit(solution)/shard_map/mid/pallas_call | solution.py:465
  144.8 0.0 copy-start
  144.8 7.7 %convolution_convert_fusion.part_ref = bf16[3584,512]{1,0:T(8,128)(2,1)S(1)} fusion(bf16[1024,3584]{1,0:T(8,128)(2,1)} %get-tuple-element.16, bf16[1024,512]{1,0:T(8,128)(2,1)S(1)} %get-tuple-element.15.ortho_ref), kind=kOutput, calls=%fused_computation | convolution fusion | flops 3759931392 | bytes 12058624 | tf_op jit(solution)/shard_map/dot_general | solution.py:879
  152.6 0.0 copy-done
  152.6 54.0 %right_sum.1 = (bf16[3584,512]{1,0:T(8,128)(2,1)S(1)}, f32[8,512]{1,0:T(8,128)S(1)}, bf16[1024,512]{1,0:T(8,128)(2,1)S(1)}, bf16[896,512]{1,0:T(8,128)(2,1)S(1)}, f32[8,512]{1,0:T(8,128)S(1)}) custom-call(bf16[3584,512]{1,0:T(8,128)(2,1)S(1)} %convolution_convert_fusion.part_ref, bf16[1024,512]{1,0:T(8,128)(2,1)S(1)} %get-tuple-element.15.ortho_ref), custom_call_target="tpu_custom_call" | custom-call | flops 10000000000 | bytes 7340032 | tf_op jit(solution)/shard_map/right_sum/pallas_call | solution.py:725
  206.6 0.0 copy-start.2
  206.6 1.8 copy-done.2
  208.5 1.1 collective-permute-start
  209.5 0.0 collective-permute-start.1
  209.5 20.6 %collective-permute-done.refs_1_ = bf16[896,512]{1,0:T(8,128)(2,1)S(1)} collective-permute-done((bf16[896,512]{1,0:T(8,128)(2,1)S(1)}, bf16[896,512]{1,0:T(8,128)(2,1)S(1)}, u32[]{:S(2)}, u32[]{:S(2)}) %collective-permute-start) | collective-permute-done | bytes 917536 | tf_op jit(solution)/shard_map/ppermute | solution.py:892
  230.1 0.0 collective-permute-start.2
  230.1 0.0 copy-start.1
  230.1 1.2 copy-done.1
  231.3 0.0 copy-start.3
  231.3 2.0 copy-done.3
  233.4 25.2 %apply_own.1 = (bf16[1,1024,3584]{2,1,0:T(8,128)(2,1)}, bf16[2,1024,3584]{2,1,0:T(8,128)(2,1)}, f32[1,1024,3584]{2,1,0:T(8,128)}, f32[1,3584,512]{2,1,0:T(8,128)}) custom-call(s32[1]{0:T(128)} %bitcast.who_ref, bf16[1,1024,3584]{2,1,0:T(8,128)(2,1)} %w_ref.1, bf16[1,1024,3584]{2,1,0:T(8,128)(2,1)} %g_ref.1, f32[1,1024,3584]{2,1,0:T(8,128)} %m_ref.1, ...), custom_call_target="tpu_custom_call" | custom-call | flops 30000001024 | bytes 66060288 | tf_op jit(solution)/shard_map/apply_own/pallas_call | solution.py:783
  258.6 0.1 stack.23.who_ref
  258.7 0.0 collective-permute-done.1.refs_2_
  258.7 0.0 collective-permute-done.2.refs_3_
  258.7 0.0 collective-permute-done.3.refs_5_
  258.7 11.8 %apply_other.1 = bf16[2,1024,3584]{2,1,0:T(8,128)(2,1)} custom-call(s32[5]{0:T(128)S(1)} %stack.23.who_ref, bf16[896,512]{1,0:T(8,128)(2,1)S(1)} %get-tuple-element.22.refs_0_, bf16[896,512]{1,0:T(8,128)(2,1)S(1)} %collective-permute-done.refs_1_, bf16[896,512]{1,0:T(8,128)(2,1)} %collective-permute-done.1.refs_2_, ...), custom_call_target="tpu_custom_call", output_to_operand_aliasing={{}: (8, {})} | custom-call | flops 3758096384 | bytes 14680064 | tf_op jit(solution)/shard_map/apply_other/pallas_call | solution.py:847
Async XLA Ops:
  0.6 258.1 %collective-permute-start.3 = (bf16[1,1024,3584]{2,1,0:T(8,128)(2,1)}, bf16[1,1024,3584]{2,1,0:T(8,128)(2,1)}, u32[]{:S(2)}, u32[]{:S(2)}) collective-permute-start(bf16[1,1024,3584]{2,1,0:T(8,128)(2,1)} %w_ref.1), channel_id=1, source_target_pairs={{0,1},{1,0},{2,3},{3,2},{4,5},{5,4},{6,7},{7,6},{8,9},{9,8},{10,11... | collective-permute-start | bytes 22020104 | tf_op jit(solution)/shard_map/ppermute | solution.py:877
  144.8 7.8 %copy-start = (bf16[1024,512]{1,0:T(8,128)(2,1)}, bf16[1024,512]{1,0:T(8,128)(2,1)S(1)}, u32[]{:S(2)}) copy-start(bf16[1024,512]{1,0:T(8,128)(2,1)S(1)} %get-tuple-element.15.ortho_ref) | copy-start | bytes 3145732
  206.6 1.8 copy-start.2
  208.5 21.7 %collective-permute-start = (bf16[896,512]{1,0:T(8,128)(2,1)S(1)}, bf16[896,512]{1,0:T(8,128)(2,1)S(1)}, u32[]{:S(2)}, u32[]{:S(2)}) collective-permute-start(bf16[896,512]{1,0:T(8,128)(2,1)S(1)} %get-tuple-element.22.refs_0_), channel_id=1, source_target_pairs={{0,16},{8,24},{16,0},{24,8},{1,17},{9,25},{17,1},{25,9},{2,18},{10... | collective-permute-start | bytes 2752520 | tf_op jit(solution)/shard_map/ppermute | solution.py:892
  209.5 49.2 %collective-permute-start.1 = (bf16[896,512]{1,0:T(8,128)(2,1)S(1)}, bf16[896,512]{1,0:T(8,128)(2,1)}, u32[]{:S(2)}, u32[]{:S(2)}) collective-permute-start(bf16[896,512]{1,0:T(8,128)(2,1)S(1)} %get-tuple-element.22.refs_0_), channel_id=1, source_target_pairs={{0,8},{8,0},{16,24},{24,16},{1,9},{9,1},{17,25},{25,17},{2,10},{10... | collective-permute-start | bytes 2752520 | tf_op jit(solution)/shard_map/ppermute | solution.py:896
  230.1 28.6 %collective-permute-start.2 = (bf16[896,512]{1,0:T(8,128)(2,1)S(1)}, bf16[896,512]{1,0:T(8,128)(2,1)}, u32[]{:S(2)}, u32[]{:S(2)}) collective-permute-start(bf16[896,512]{1,0:T(8,128)(2,1)S(1)} %collective-permute-done.refs_1_), channel_id=1, source_target_pairs={{0,8},{8,0},{16,24},{24,16},{1,9},{9,1},{17,25},{25,17},{2,10},{10... | collective-permute-start | bytes 2752520 | tf_op jit(solution)/shard_map/ppermute | solution.py:896
  230.1 1.2 copy-start.1
  231.3 2.0 copy-start.3
